TPU v7x, 128 devices: a whole 4x4x4 slice. The times are simulated.
128 devices in a mesh: dp: 1, ep: 128 (over z, y, x, core).
Axes of the slice: x: 4, y: 4, z: 4, core: 2. Of those that a mesh axis runs over, the one named last changes fastest.
Arguments:
- tokens: bfloat16 [65536, 1024], P(('dp', 'ep'))
- slot_ids: int32 [65536, 4, 32], P(('dp', 'ep'))
- request_rows: int32 [128, 128, 64], P(('dp', 'ep'))
- gate_vals: float32 [65536, 4, 32], P(('dp', 'ep'))
- grad_out: bfloat16 [65536, 1024], P(('dp', 'ep'))
- table_up: bfloat16 [16384, 1024], P('ep')
- table_down: bfloat16 [16384, 1024], P('ep')
Outputs:
- output 1: bfloat16 [65536, 1024], P(('dp', 'ep'))
- output 2: bfloat16 [65536, 1024], P(('dp', 'ep'))
- output 3: bfloat16 [16384, 1024], P(('dp', 'ep'))
- output 4: bfloat16 [16384, 1024], P(('dp', 'ep'))
All inputs are finite; a program needn't handle non-finite values.
Results may differ from a plain program's by a relative error of at most 0.00849675.
Values are sent between devices in bfloat16 or wider.
A program may use at most 1 GiB of HBM per device.

v0:
```python
import functools
import math
import jax
import jax.numpy as jnp
from jax import lax
from jax.experimental import pallas as pl
from jax.experimental.pallas import tpu as pltpu
from jax.sharding import PartitionSpec as P


CORE, ZTOK, ZTAB = 1, 32, 96
N_EP, ROWS, REQ = 128, 128, 64
N_SET = 4
N_OWN = 32
N_GRP = N_OWN // 4
N_HI = N_OWN * REQ // 128
F32, BF16 = jnp.float32, jnp.bfloat16
NT = (((1,), (1,)), ((), ()))


def gelu_pair(pre_act):
    normal_cdf = 0.5 * (1.0 + lax.erf(pre_act * (2.0 ** -0.5)))
    normal_pdf = jnp.exp(-0.5 * pre_act * pre_act) * ((2.0 * math.pi) ** -0.5)
    return pre_act * normal_cdf, normal_cdf + pre_act * normal_pdf


def dot(a, b, dims=(((1,), (0,)), ((), ()))):
    return lax.dot_general(a, b, dims, preferred_element_type=F32)


def gate_kernel(ctl_ref, slot_ref, gate_ref, out_ref, hi_ref, lo_ref, g1_ref, g2_ref, g3_ref):
    n_tok = slot_ref.shape[0]
    slot = slot_ref[...].astype(jnp.int32)
    owner = slot >> 6
    z_of = owner >> 5
    here = ((owner & 1) == ctl_ref[0]) & ((((z_of + 1) >> 1) & 1) == ctl_ref[1])
    local = ((((owner >> 1) & 15) * 2 + (z_of >> 1)) << 6) + (slot & 63)
    hi_ref[...] = jnp.where(here, local >> 7, 255).astype(F32)
    lo_ref[...] = (local & 127).astype(F32)
    gate = gate_ref[...]
    g1 = gate.astype(BF16).astype(F32)
    g2 = (gate - g1).astype(BF16).astype(F32)
    g1_ref[...] = g1
    g2_ref[...] = g2
    g3_ref[...] = (gate - g1) - g2
    row_iota = lax.broadcasted_iota(jnp.int32, (16, 128), 0).astype(F32)
    iotas = [(row_iota + 16.0 * k).astype(BF16) for k in range(8)]
    out_flat = out_ref.reshape(n_tok * N_HI, 128)

    def spread(ref, t):
        return jnp.broadcast_to(ref[pl.ds(t, 1), :], (16, 128)).astype(BF16)

    def sides(t):
        hit = spread(hi_ref, t) == iotas[0]
        lhs = jnp.concatenate([jnp.where(hit, spread(ref, t), jnp.zeros((16, 128), BF16)) for ref in (g1_ref, g2_ref, g3_ref)], axis=0)
        lo_row = spread(lo_ref, t)
        rhs = jnp.concatenate([jnp.where(lo_row == one_iota, jnp.ones((16, 128), BF16), jnp.zeros((16, 128), BF16)) for one_iota in iotas], axis=0)
        return lhs, rhs

    def two_tokens(t):
        lhs_a, rhs_a = sides(t)
        lhs_b, rhs_b = sides(t + 1)
        empty = jnp.zeros_like(lhs_a)
        lhs = jnp.concatenate([jnp.concatenate([lhs_a, empty], axis=1), jnp.concatenate([empty, lhs_b], axis=1)], axis=0)
        res = dot(lhs, jnp.concatenate([rhs_a, rhs_b], axis=1), NT)
        return (res[32:48] + res[16:32]) + res[:16], (res[80:96] + res[64:80]) + res[48:64]

    def body(step, carry):
        for k in range(0, tok_step, 2):
            row_a, row_b = two_tokens(step * tok_step + k)
            base = (step * (tok_step // 8) + k // 8) * (8 * N_HI) + k % 8
            out_flat[pl.ds(base, N_HI, stride=8), :] = row_a
            out_flat[pl.ds(base + 1, N_HI, stride=8), :] = row_b
        return carry

    tok_step = min(64, n_tok)
    lax.fori_loop(0, n_tok // tok_step, body, 0)


def gate_matrix(ctl, meta, n_tok):
    tok_blk = min(256, n_tok)
    n_blk = n_tok // tok_blk
    return pl.pallas_call(
        gate_kernel,
        grid=(n_blk,),
        in_specs=[
            pl.BlockSpec(memory_space=pltpu.SMEM),
            pl.BlockSpec((tok_blk, 128), lambda i: (i, 0)),
            pl.BlockSpec((tok_blk, 128), lambda i: (i + n_blk, 0)),
        ],
        out_specs=pl.BlockSpec((tok_blk // 8, N_HI, 8, 128), lambda i: (i, 0, 0, 0)),
        out_shape=jax.ShapeDtypeStruct((n_tok // 8, N_HI, 8, 128), F32),
        scratch_shapes=[pltpu.VMEM((tok_blk, 128), F32)] * 5,
        compiler_params=pltpu.CompilerParams(vmem_limit_bytes=60 * 2 ** 20),
        cost_estimate=pl.CostEstimate(flops=n_tok * 12 * 2 ** 20, bytes_accessed=n_tok * 9216, transcendentals=0),
        name="gate_matrix",
    )(ctl, meta, meta)


def pick_rows(p_ref, table_ref, out_ref):
    for i in range(2):
        rows = dot(p_ref[0, i], table_ref[i * 256:(i + 1) * 256, :]).astype(BF16)
        for s in range(N_SET):
            out_ref[0, s, i * 128:(i + 1) * 128, :] = rows[s * 128:(s + 1) * 128]


def halves(n_tok):
    half = max(n_tok // 2, 16)
    return [slice(t, t + half) for t in range(0, n_tok, half)]


def first_kernel(n_tok, u_ref, p_ref, pt_ref, *refs):
    g_refs, x_refs, dy_refs = (refs[i * N_SET:(i + 1) * N_SET] for i in range(3))
    uc_ref, w_ref, s_ref, dv_ref, wrt, pre = refs[3 * N_SET:]
    tok_chunk = min(64, n_tok)

    def front(s):
        for part in halves(n_tok):
            pre[s, part, :] = dot(x_refs[s][part, :], uc_ref[0, s], NT)

    def back(s):
        for t0 in range(0, n_tok, tok_chunk):
            row0 = s * n_tok + t0
            for i in range(2):
                gate = g_refs[s][t0 // 8:(t0 + tok_chunk) // 8, i].reshape(tok_chunk, 128)
                act, slope = gelu_pair(pre[s, t0:t0 + tok_chunk, i * 128:(i + 1) * 128])
                used = gate > 0.0
                w_ref[row0:row0 + tok_chunk, i * 128:(i + 1) * 128] = jnp.where(used, gate * act, 0.0).astype(BF16)
                s_ref[row0:row0 + tok_chunk, i * 128:(i + 1) * 128] = jnp.where(used, gate * slope, 0.0)
        for i in range(2):
            wrt[i * 256:(i + 1) * 256, s * n_tok:(s + 1) * n_tok] = dot(pt_ref[0, s, i], w_ref[s * n_tok:(s + 1) * n_tok, i * 128:(i + 1) * 128], NT).astype(BF16)

    pick_rows(p_ref, u_ref, uc_ref)
    front(0)
    for s in range(1, N_SET):
        front(s)
        back(s - 1)
    back(N_SET - 1)
    dy_all = jnp.concatenate([ref[...] for ref in dy_refs], axis=0)
    dv_ref[...] = dot(wrt[...], dy_all).astype(BF16)


def whole(arr):
    return pl.BlockSpec(arr.shape, lambda g: (0,) * arr.ndim, pipeline_mode=pl.Buffered(1))


def first_pass(u_all, p_hot, pt_hot, gates, xs, dys):
    n_tok, width = xs[0].shape
    all_tok = N_SET * n_tok
    flops = 2 * N_GRP * N_SET * (256 * 256 * width + n_tok * width * 256 + n_tok * 128 * 512 + n_tok * 512 * width)
    return pl.pallas_call(
        functools.partial(first_kernel, n_tok),
        grid=(N_GRP,),
        in_specs=[
            pl.BlockSpec((512, width), lambda g: (g, 0)),
            pl.BlockSpec((1, 2, N_SET * 128, 256), lambda g: (g, 0, 0, 0)),
            pl.BlockSpec((1, N_SET, 2, 256, 128), lambda g: (g, 0, 0, 0, 0)),
        ] + [pl.BlockSpec((n_tok // 8, 2, 8, 128), lambda g: (0, g, 0, 0))] * N_SET + [whole(one) for one in (*xs, *dys)],
        out_specs=[
            pl.BlockSpec((1, N_SET, 256, width), lambda g: (g, 0, 0, 0)),
            pl.BlockSpec((all_tok, 256), lambda g: (0, g)),
            pl.BlockSpec((all_tok, 256), lambda g: (0, g)),
            pl.BlockSpec((512, width), lambda g: (g, 0)),
        ],
        out_shape=[
            jax.ShapeDtypeStruct((N_GRP, N_SET, 256, width), BF16),
            jax.ShapeDtypeStruct((all_tok, N_GRP * 256), BF16),
            jax.ShapeDtypeStruct((all_tok, N_GRP * 256), F32),
            jax.ShapeDtypeStruct((N_GRP * 512, width), BF16),
        ],
        scratch_shapes=[pltpu.VMEM((512, all_tok), BF16), pltpu.VMEM((N_SET, n_tok, 256), F32)],
        compiler_params=pltpu.CompilerParams(vmem_limit_bytes=60 * 2 ** 20),
        cost_estimate=pl.CostEstimate(flops=flops, bytes_accessed=76 * 2 ** 20, transcendentals=all_tok * N_GRP * 256),
        name="first_pass",
    )(u_all, p_hot, pt_hot, *gates, *xs, *dys)


def down_kernel(n_tok, v_ref, p_ref, w_ref, vc_ref, y_ref):
    @pl.when(pl.program_id(0) == 0)
    def _():
        y_ref[...] = jnp.zeros_like(y_ref)

    pick_rows(p_ref, v_ref, vc_ref)
    for s in range(N_SET):
        y_ref[s * n_tok:(s + 1) * n_tok, :] += dot(w_ref[s * n_tok:(s + 1) * n_tok, :], vc_ref[0, s])


def down_pass(v_all, p_hot, w_all):
    width = v_all.shape[1]
    all_tok = w_all.shape[0]
    n_tok = all_tok // N_SET
    flops = 2 * N_GRP * N_SET * (256 * 256 * width + n_tok * width * 256)
    return pl.pallas_call(
        functools.partial(down_kernel, n_tok),
        grid=(N_GRP,),
        in_specs=[
            pl.BlockSpec((512, width), lambda g: (g, 0)),
            pl.BlockSpec((1, 2, N_SET * 128, 256), lambda g: (g, 0, 0, 0)),
            pl.BlockSpec((all_tok, 256), lambda g: (0, g)),
        ],
        out_specs=[
            pl.BlockSpec((1, N_SET, 256, width), lambda g: (g, 0, 0, 0)),
            pl.BlockSpec((all_tok, width), lambda g: (0, 0)),
        ],
        out_shape=[
            jax.ShapeDtypeStruct((N_GRP, N_SET, 256, width), BF16),
            jax.ShapeDtypeStruct((all_tok, width), F32),
        ],
        compiler_params=pltpu.CompilerParams(vmem_limit_bytes=60 * 2 ** 20),
        cost_estimate=pl.CostEstimate(flops=flops, bytes_accessed=44 * 2 ** 20, transcendentals=0),
        name="down_pass",
    )(v_all, p_hot, w_all)


def second_kernel(n_tok, vc_ref, pt_ref, s_ref, *refs):
    x_refs, dy_refs = refs[:N_SET], refs[N_SET:2 * N_SET]
    c_ref, du_ref, crt = refs[2 * N_SET:]

    def front(s):
        for part in halves(n_tok):
            rows = slice(s * n_tok + part.start, s * n_tok + part.stop)
            back = dot(dy_refs[s][part, :], vc_ref[0, s], NT)
            slope = s_ref[rows, :]
            c_ref[rows, :] = jnp.where(slope == 0.0, 0.0, slope * back).astype(BF16)

    def back(s):
        rows = slice(s * n_tok, (s + 1) * n_tok)
        for i in range(2):
            crt[i * 256:(i + 1) * 256, rows] = dot(pt_ref[0, s, i], c_ref[rows, i * 128:(i + 1) * 128], NT).astype(BF16)

    front(0)
    for s in range(1, N_SET):
        front(s)
        back(s - 1)
    back(N_SET - 1)
    x_all = jnp.concatenate([ref[...] for ref in x_refs], axis=0)
    du_ref[...] = dot(crt[...], x_all).astype(BF16)


def second_pass(vc, pt_hot, slopes, xs, dys):
    n_tok, width = xs[0].shape
    all_tok = N_SET * n_tok
    flops = 2 * N_GRP * N_SET * (n_tok * width * 256 + n_tok * 128 * 512 + n_tok * 512 * width)
    return pl.pallas_call(
        functools.partial(second_kernel, n_tok),
        grid=(N_GRP,),
        in_specs=[
            pl.BlockSpec((1, N_SET, 256, width), lambda g: (g, 0, 0, 0)),
            pl.BlockSpec((1, N_SET, 2, 256, 128), lambda g: (g, 0, 0, 0, 0)),
            pl.BlockSpec((all_tok, 256), lambda g: (0, g)),
        ] + [whole(one) for one in (*xs, *dys)],
        out_specs=[
            pl.BlockSpec((all_tok, 256), lambda g: (0, g)),
            pl.BlockSpec((512, width), lambda g: (g, 0)),
        ],
        out_shape=[
            jax.ShapeDtypeStruct((all_tok, N_GRP * 256), BF16),
            jax.ShapeDtypeStruct((N_GRP * 512, width), BF16),
        ],
        scratch_shapes=[pltpu.VMEM((512, all_tok), BF16)],
        compiler_params=pltpu.CompilerParams(vmem_limit_bytes=60 * 2 ** 20),
        cost_estimate=pl.CostEstimate(flops=flops, bytes_accessed=58 * 2 ** 20, transcendentals=0),
        name="second_pass",
    )(vc, pt_hot, slopes, *xs, *dys)


def token_grad_kernel(c_ref, uc_ref, dx_ref):
    width = uc_ref.shape[-1]
    dx_ref[...] = dot(c_ref[...], uc_ref[...].reshape(N_GRP * 256, width))


def token_grad(c_all, uc, first_set):
    width = uc.shape[-1]
    n_tok = c_all.shape[0] // N_SET
    flops = 2 * 2 * n_tok * N_GRP * 256 * width
    return pl.pallas_call(
        token_grad_kernel,
        grid=(2,),
        in_specs=[
            pl.BlockSpec((n_tok, N_GRP * 256), lambda i: (first_set + i, 0)),
            pl.BlockSpec((N_GRP, 1, 256, width), lambda i: (0, first_set + i, 0, 0)),
        ],
        out_specs=pl.BlockSpec((n_tok, width), lambda i: (i, 0)),
        out_shape=jax.ShapeDtypeStruct((2 * n_tok, width), F32),
        compiler_params=pltpu.CompilerParams(vmem_limit_bytes=60 * 2 ** 20),
        cost_estimate=pl.CostEstimate(flops=flops, bytes_accessed=16 * 2 ** 20, transcendentals=0),
        name="token_grad",
    )(c_all, uc)


def ring_place():
    me = lax.axis_index('ep')
    core, x_me, y_me, z_me = me % 2, (me // 2) % 4, (me // 8) % 4, me // 32

    def device(z, y, x):
        return ((z * 4 + y) * 4 + x) * 2 + core

    return x_me, y_me, z_me, device


def meet(peers):
    barrier = pltpu.get_barrier_semaphore()
    for peer in peers:
        pl.semaphore_signal(barrier, inc=1, device_id={'ep': peer}, device_id_type=pl.DeviceIdType.MESH)
    pl.semaphore_wait(barrier, len(peers))


HALF_A, HALF_B, N_MSG = (2, 1), (3, 0), 19


def reduce_kernel(part_ref, out_ref, s1_prev, s1_next, s2_prev, s2_next, sum_next, sum_prev, mid, t1_prev, t1_next, t2_prev, t2_next, tsum_next, tsum_prev, keep, z_send, z_recv, send_sem, recv_sem):
    rows, width = out_ref.shape
    half = width // 2
    x_me, y_me, z_me, device = ring_place()
    z_peer = device(3 - z_me, y_me, x_me)
    upper = z_me // 2
    x_next, x_prev = device(z_me, y_me, (x_me + 1) % 4), device(z_me, y_me, (x_me + 3) % 4)
    y_next, y_prev = device(z_me, (y_me + 1) % 4, x_me), device(z_me, (y_me + 3) % 4, x_me)
    meet((x_next, x_prev, y_next, y_prev, z_peer))
    chunk = 32

    def add_up(n_rows, store, *loads):
        def step(i, carry):
            at = pl.ds(pl.multiple_of(i * chunk, chunk), chunk)
            total = loads[0](i, at)
            for load in loads[1:]:
                total = total + load(i, at)
            store(at, total)
            return carry

        lax.fori_loop(0, n_rows // chunk, step, 0)

    def from_buf(buf, *index):
        return lambda i, at: buf[(*index, at, slice(None))].astype(F32)

    def into_buf(buf, *index):
        def store(at, total):
            buf[(*index, at, slice(None))] = total.astype(buf.dtype)

        return store

    class Side:
        pass

    sides = []
    for k in range(2):
        one = Side()
        one.k = k
        first, second = (x_me, y_me) if k == 0 else (y_me, x_me)
        one.first, one.second = first, second
        one.next1, one.prev1 = (x_next, x_prev) if k == 0 else (y_next, y_prev)
        one.next2, one.prev2 = (y_next, y_prev) if k == 0 else (x_next, x_prev)
        sides.append(one)

    def start_of(one, shift1, shift2):
        first, second = (one.first + shift1) % 4, (one.second + shift2) % 4
        chip = second * 4 + first if one.k == 0 else first * 4 + second
        return chip * (2 * rows)

    def own(one, shift1, shift2):
        return part_ref.at[pl.ds(pl.multiple_of(start_of(one, shift1, shift2), 2 * rows), 2 * rows), pl.ds(one.k * half, half)]

    def load_own(one, shift1, shift2):
        start = start_of(one, shift1, shift2)
        return lambda i, at: part_ref[pl.ds(pl.multiple_of(start + i * chunk, chunk), chunk), one.k * half:(one.k + 1) * half].astype(F32)

    def message(one, number, src, dst, peer):
        return pltpu.make_async_remote_copy(
            src_ref=src, dst_ref=dst, send_sem=send_sem.at[one.k, number], recv_sem=recv_sem.at[one.k, number],
            device_id={'ep': peer}, device_id_type=pl.DeviceIdType.MESH)

    for one in sides:
        k = one.k
        one.s1n = [message(one, i, own(one, 2, HALF_A[i]), s1_prev.at[k, i], one.next1) for i in range(2)]
        one.s1p = [message(one, 2 + i, own(one, 2, HALF_B[i]), s1_next.at[k, i], one.prev1) for i in range(2)]
        one.inn = [message(one, 4 + i, own(one, 1, HALF_B[i]), s2_prev.at[k, HALF_B[i]], one.next1) for i in range(2)]
        one.inp = [message(one, 6 + i, own(one, 3, HALF_A[i]), s2_next.at[k, HALF_A[i]], one.prev1) for i in range(2)]
        one.dpn = [message(one, 8 + i, sum_next.at[k, i], s2_prev.at[k, HALF_A[i]], one.next1) for i in range(2)]
        one.dpp = [message(one, 10 + i, sum_prev.at[k, i], s2_next.at[k, HALF_B[i]], one.prev1) for i in range(2)]
        lower_rows, upper_rows = pl.ds(0, rows), pl.ds(rows, rows)
        one.t1n = message(one, 12, mid.at[k, 2, lower_rows], t1_prev.at[k], one.next2)
        one.t1p = message(one, 13, mid.at[k, 2, upper_rows], t1_next.at[k], one.prev2)
        one.tin = message(one, 14, mid.at[k, 1, upper_rows], t2_prev.at[k, 1], one.next2)
        one.tip = message(one, 15, mid.at[k, 3, lower_rows], t2_next.at[k, 0], one.prev2)
        one.tdn = message(one, 16, tsum_next.at[k], t2_prev.at[k, 0], one.next2)
        one.tdp = message(one, 17, tsum_prev.at[k], t2_next.at[k, 1], one.prev2)
        one.zz = message(one, 18, z_send.at[k], z_recv.at[k], z_peer)

    for i in range(2):
        for one in sides:
            one.s1n[i].start()
            one.s1p[i].start()
    for i in range(2):
        for one in sides:
            one.inn[i].start()
            one.inp[i].start()
    for i in range(2):
        for one in sides:
            one.s1n[i].wait_recv()
            add_up(2 * rows, into_buf(sum_next, one.k, i), load_own(one, 1, HALF_A[i]), from_buf(s1_prev, one.k, i))
            one.dpn[i].start()
            one.s1p[i].wait_recv()
            add_up(2 * rows, into_buf(sum_prev, one.k, i), load_own(one, 3, HALF_B[i]), from_buf(s1_next, one.k, i))
            one.dpp[i].start()
    for i, r in ((0, 2), (0, 3), (1, 1), (1, 0)):
        for one in sides:
            k = one.k
            if r in HALF_A:
                one.inp[i].wait_recv()
                one.dpn[i].wait_recv()
            else:
                one.inn[i].wait_recv()
                one.dpp[i].wait_recv()
            add_up(2 * rows, into_buf(mid, k, r), load_own(one, 0, r), from_buf(s2_prev, k, r), from_buf(s2_next, k, r))
            if r == 2:
                one.t1n.start()
                one.t1p.start()
            if r == 3:
                one.tip.start()
            if r == 1:
                one.tin.start()
    for one in sides:
        k = one.k
        one.t1n.wait_recv()
        add_up(rows, into_buf(tsum_next, k), from_buf(mid, k, 1), from_buf(t1_prev, k))
        one.tdn.start()
        one.t1p.wait_recv()
        add_up(rows, into_buf(tsum_prev, k), lambda i, at: mid[k, 3, pl.ds(pl.multiple_of(rows + i * chunk, chunk), chunk), :].astype(F32), from_buf(t1_next, k))
        one.tdp.start()
    for one in sides:
        k = one.k
        one.tin.wait_recv()
        one.tip.wait_recv()
        one.tdn.wait_recv()
        one.tdp.wait_recv()

        def last_sum(i, carry, k=k):
            at = pl.ds(pl.multiple_of(i * chunk, chunk), chunk)
            low = mid[k, 0, at, :].astype(F32) + t2_prev[k, 0, at, :].astype(F32) + t2_next[k, 0, at, :].astype(F32)
            high = mid[k, 0, pl.ds(pl.multiple_of(rows + i * chunk, chunk), chunk), :].astype(F32) + t2_prev[k, 1, at, :].astype(F32) + t2_next[k, 1, at, :].astype(F32)
            keep[k, at, :] = jnp.where(upper == 1, high, low)
            z_send[k, at, :] = jnp.where(upper == 1, low, high).astype(BF16)
            return carry

        lax.fori_loop(0, rows // chunk, last_sum, 0)
        one.zz.start()
    for one in sides:
        k = one.k
        one.zz.wait_recv()

        def store_out(at, total, k=k):
            out_ref[at, k * half:(k + 1) * half] = total.astype(BF16)

        add_up(rows, store_out, from_buf(keep, k), from_buf(z_recv, k))
    for one in sides:
        for msg in one.s1n + one.s1p + one.inn + one.inp + one.dpn + one.dpp + [one.t1n, one.t1p, one.tin, one.tip, one.tdn, one.tdp, one.zz]:
            msg.wait_send()


def reduce_rows(part):
    width = part.shape[1]
    rows = part.shape[0] // N_OWN
    half = width // 2
    big, small = (2 * rows, half), (rows, half)
    vmem = pl.BlockSpec(memory_space=pltpu.VMEM)
    return pl.pallas_call(
        reduce_kernel,
        in_specs=[vmem],
        out_specs=vmem,
        out_shape=jax.ShapeDtypeStruct((rows, width), BF16),
        scratch_shapes=[pltpu.VMEM(shape, BF16) for shape in ((2, 2, *big), (2, 2, *big), (2, 4, *big), (2, 4, *big), (2, 2, *big), (2, 2, *big), (2, 4, *big), (2, *small), (2, *small), (2, 2, *small), (2, 2, *small), (2, *small), (2, *small))]
        + [pltpu.VMEM((2, *small), F32), pltpu.VMEM((2, *small), BF16), pltpu.VMEM((2, *small), BF16), pltpu.SemaphoreType.DMA((2, N_MSG)), pltpu.SemaphoreType.DMA((2, N_MSG))],
        compiler_params=pltpu.CompilerParams(collective_id=0, has_side_effects=True, vmem_limit_bytes=48 * 2 ** 20),
        cost_estimate=pl.CostEstimate(flops=10 ** 9, bytes_accessed=part.size * 4, transcendentals=0),
        name="reduce_rows",
    )(part)


def hot_tables(req_sets, core, zgrp):
    yx = jnp.arange(16)[:, None]
    z_of = jnp.where(zgrp == 0, jnp.array([0, 3]), jnp.array([1, 2]))[None, :]
    owners = ((z_of * 16 + yx) * 2 + core).reshape(N_OWN)
    req = jnp.stack([one[owners] for one in req_sets], axis=1)
    req = req.reshape(N_GRP, 2, 2, N_SET, REQ).transpose(0, 3, 1, 2, 4)
    row = (req + ROWS * jnp.arange(2)[:, None]).reshape(N_GRP, N_SET, 2, 2 * REQ)
    ids = jnp.arange(2 * ROWS)
    pt_hot = (row[..., None, :] == ids[:, None]).astype(BF16)
    p_hot = (row.transpose(0, 2, 1, 3).reshape(N_GRP, 2, N_SET * 128)[..., None] == ids).astype(BF16)
    return p_hot, pt_hot


def solution(mesh):
    tok_spec = P(('dp', 'ep'))
    table_spec = P('ep')
    plane = [[z * 32 + yx * 2 + c for yx in range(16)] for z in range(4) for c in range(2)]

    def swap(arr, mask):
        return lax.ppermute(arr, 'ep', [(i, i ^ mask) for i in range(N_EP)])

    def device_part(tokens, slot_ids, request_rows, gate_vals, grad_out, up_local, down_local):
        n_tok, _ = tokens.shape
        n_sel = slot_ids.shape[1] * slot_ids.shape[2]
        index = lax.axis_index('ep')
        core, z_me = index % 2, index // 32
        zgrp = ((z_me + 1) // 2) % 2

        def table_rows(local):
            other = swap(local, ZTAB)
            both = jnp.where(z_me < 2, jnp.concatenate([local, other]), jnp.concatenate([other, local]))
            return lax.all_gather(both, 'ep', axis=0, tiled=True, axis_index_groups=plane)

        def grad_rows(part):
            mine = lax.psum_scatter(part, 'ep', scatter_dimension=0, tiled=True, axis_index_groups=plane)
            keep = lax.dynamic_slice_in_dim(mine, (z_me // 2) * ROWS, ROWS)
            give = lax.dynamic_slice_in_dim(mine, (1 - z_me // 2) * ROWS, ROWS)
            return (keep.astype(F32) + swap(give, ZTAB).astype(F32)).astype(BF16)

        def for_other_chip(remote_part):
            return remote_part[:n_tok] + swap(remote_part[n_tok:], CORE)

        def collect(local_part, from_z):
            from_core = swap(local_part[n_tok:], CORE)
            return (local_part[:n_tok] + from_core + from_z).astype(BF16)

        n_req = request_rows.shape[1] * request_rows.shape[2] // n_sel
        meta0 = jnp.concatenate([slot_ids.reshape(n_tok, n_sel).astype(F32), gate_vals.reshape(n_tok, n_sel), request_rows.reshape(n_req, n_sel).astype(F32)])
        meta2 = swap(meta0, ZTOK)
        meta1 = swap(meta0, CORE)
        meta3 = swap(meta2, CORE)
        x2 = swap(tokens, ZTOK)
        dy2 = swap(grad_out, ZTOK)
        u_all = table_rows(up_local)
        v_all = table_rows(down_local)
        xs = (tokens, swap(tokens, CORE), x2, swap(x2, CORE))
        dys = (grad_out, swap(grad_out, CORE), dy2, swap(dy2, CORE))
        metas = (meta0, meta1, meta2, meta3)
        p_hot, pt_hot = hot_tables([m[2 * n_tok:].reshape(N_EP, REQ).astype(jnp.int32) for m in metas], core, zgrp)

        ctl = jnp.stack([core, zgrp]).astype(jnp.int32)
        gates = []
        for meta in metas:
            gates.append(gate_matrix(ctl, meta, n_tok))
        uc, w_all, slopes, dv_part = first_pass(u_all, p_hot, pt_hot, gates, xs, dys)
        vc, y_part = down_pass(v_all, p_hot, w_all)
        y_for_z, vc = lax.optimization_barrier((for_other_chip(y_part[2 * n_tok:]), vc))
        y_from_z = swap(y_for_z, ZTOK)
        c_all, du_part = second_pass(vc, pt_hot, slopes, xs, dys)
        dx_rem = token_grad(c_all, uc, 2)
        dx_loc = token_grad(c_all, uc, 0)
        y = collect(y_part[:2 * n_tok], y_from_z)
        grad_down = grad_rows(dv_part)
        grad_up = reduce_rows(du_part)
        dx = collect(dx_loc, swap(for_other_chip(dx_rem), ZTOK))
        return y, dx, grad_up, grad_down

    return jax.shard_map(device_part, mesh=mesh, in_specs=(tok_spec, tok_spec, tok_spec, tok_spec, tok_spec, table_spec, table_spec), out_specs=(tok_spec, tok_spec, tok_spec, tok_spec), check_vma=False)
```

profile of v0, /device:TPU:11, one launch (start us, length us, event | category | flops | bytes accessed | tf_op | source)
XLA Modules:
  0.0 350.6 jit_solution(13105975730834668301)
XLA Ops:
  7.2 0.0 all-gather.5.cloned.1.call-start
  7.2 3.8 %collective-permute-start.4 = (bf16[128,1024]{1,0:T(8,128)(2,1)}, bf16[128,1024]{1,0:T(8,128)(2,1)S(1)}, u32[]{:S(2)}, u32[]{:S(2)}) collective-permute-start(bf16[128,1024]{1,0:T(8,128)(2,1)} %param.14), channel_id=1, source_target_pairs={{0,96},{1,97},{2,98},{3,99},{4,100},{5,101},{6,102},{7,103},{8,104... | collective-permute-start | bytes 786440 | tf_op jit(solution)/shard_map/ppermute | solution.py:498
  11.1 6.2 %collective-permute-done.4 = bf16[128,1024]{1,0:T(8,128)(2,1)S(1)} collective-permute-done((bf16[128,1024]{1,0:T(8,128)(2,1)}, bf16[128,1024]{1,0:T(8,128)(2,1)S(1)}, u32[]{:S(2)}, u32[]{:S(2)}) %collective-permute-start.4) | collective-permute-done | bytes 262176 | tf_op jit(solution)/shard_map/ppermute | solution.py:498
  17.3 2.0 maximum_select_fusion.1
  19.3 0.0 all-gather.3.cloned.1.call-start
  19.4 2.5 collective-permute-start
  21.8 5.6 %collective-permute-done = bf16[128,1024]{1,0:T(8,128)(2,1)S(1)} collective-permute-done((bf16[128,1024]{1,0:T(8,128)(2,1)}, bf16[128,1024]{1,0:T(8,128)(2,1)S(1)}, u32[]{:S(2)}, u32[]{:S(2)}) %collective-permute-start) | collective-permute-done | bytes 262176 | tf_op jit(solution)/shard_map/ppermute | solution.py:498
  27.5 2.0 maximum_select_fusion
  29.5 0.0 reduce-scatter.2.cloned.1.call-start
  29.6 0.1 copy.17
  29.7 0.1 convert_element_type.64
  29.8 0.1 copy.18
  29.9 0.1 copy.19
  30.1 0.1 collective-permute-start.2
  30.2 2.2 collective-permute-start.1
  32.4 1.7 collective-permute-start.6
  34.1 0.3 collective-permute-start.5
  34.3 0.6 pad_add_fusion.ctl_ref
  34.9 8.6 %gate_matrix.4.refs_0_ = f32[64,16,8,128]{3,2,1,0:T(8,128)} custom-call(s32[2]{0:T(128)} %pad_add_fusion.ctl_ref, f32[1088,128]{1,0:T(8,128)} %copy-done.1, f32[1088,128]{1,0:T(8,128)} %copy-done.1), custom_call_target="tpu_custom_call" | custom-call | flops 6442450944 | bytes 4718592 | tf_op jit(solution)/shard_map/gate_matrix/pallas_call | solution.py:83
  43.6 0.1 add.113
  43.7 0.6 gather_fusion
  44.3 0.6 collective-permute-start.8
  44.9 0.1 convert_element_type.66
  44.9 0.6 gather_fusion.1
  45.6 0.1 convert_element_type.68
  45.6 0.6 gather_fusion.2
  46.2 2.3 collective-permute-start.3
  48.5 8.6 %gate_matrix.5.refs_1_ = f32[64,16,8,128]{3,2,1,0:T(8,128)} custom-call(s32[2]{0:T(128)} %pad_add_fusion.ctl_ref, f32[1088,128]{1,0:T(8,128)} %copy-done.7, f32[1088,128]{1,0:T(8,128)} %copy-done.7), custom_call_target="tpu_custom_call" | custom-call | flops 6442450944 | bytes 4718592 | tf_op jit(solution)/shard_map/gate_matrix/pallas_call | solution.py:83
  57.2 8.6 %gate_matrix.6.refs_2_ = f32[64,16,8,128]{3,2,1,0:T(8,128)} custom-call(s32[2]{0:T(128)} %pad_add_fusion.ctl_ref, f32[1088,128]{1,0:T(8,128)} %copy-done.6, f32[1088,128]{1,0:T(8,128)} %copy-done.6), custom_call_target="tpu_custom_call" | custom-call | flops 6442450944 | bytes 4718592 | tf_op jit(solution)/shard_map/gate_matrix/pallas_call | solution.py:83
  65.8 21.5 %collective-permute-done.9.refs_10_.refs_6_ = bf16[512,1024]{1,0:T(8,128)(2,1)} collective-permute-done((bf16[512,1024]{1,0:T(8,128)(2,1)}, bf16[512,1024]{1,0:T(8,128)(2,1)}, u32[]{:S(2)}, u32[]{:S(2)}) %collective-permute-start.9) | collective-permute-done | bytes 1048608 | tf_op jit(solution)/shard_map/ppermute | solution.py:498
  87.3 3.0 collective-permute-start.10
  90.3 0.1 convert_element_type.70
  90.4 0.6 gather_fusion.3
  91.0 0.1 fusion.4
  91.1 0.1 reshape.121
  91.2 3.3 fusion.1.pt_ref
  94.5 3.7 %fusion.p_ref = bf16[8,2,512,256]{3,2,1,0:T(8,128)(2,1)} fusion(s32[8,2,512]{2,1,0:T(2,128)S(1)} %bitcast.21), kind=kLoop, calls=%fused_computation.6 | loop fusion | flops 4194304 | bytes 4227072 | tf_op jit(solution)/shard_map/convert_element_type | solution.py:488
  98.2 8.6 %gate_matrix.7.refs_3_ = f32[64,16,8,128]{3,2,1,0:T(8,128)} custom-call(s32[2]{0:T(128)} %pad_add_fusion.ctl_ref, f32[1088,128]{1,0:T(8,128)} %copy-done.8, f32[1088,128]{1,0:T(8,128)} %copy-done.8), custom_call_target="tpu_custom_call" | custom-call | flops 6442450944 | bytes 4718592 | tf_op jit(solution)/shard_map/gate_matrix/pallas_call | solution.py:83
  106.8 51.3 %first_pass.1 = (bf16[8,4,256,1024]{3,2,1,0:T(8,128)(2,1)}, bf16[2048,2048]{1,0:T(8,128)(2,1)}, f32[2048,2048]{1,0:T(8,128)}, bf16[4096,1024]{1,0:T(8,128)(2,1)}) custom-call(bf16[4096,1024]{1,0:T(8,128)(2,1)} %all-gather.5.cloned.1.call-done.u_ref, bf16[8,2,512,256]{3,2,1,0:T(8,128)(2,1)} %fusion.p_ref, bf16[8,4,2,256,128]{4,3,2,1,0:T(8,128)(2,1)} %fusion.1.pt_ref, ...), custom_call_target="tpu_custom_call" | custom-call | flops 32212254720 | bytes 79691776 | tf_op jit(solution)/shard_map/first_pass/pallas_call | solution.py:151
  158.1 4.9 %all-gather.3.cloned.1.call-done.v_ref = bf16[4096,1024]{1,0:T(8,128)(2,1)} async-done(((bf16[256,1024]{1,0:T(8,128)(2,1)}), bf16[4096,1024]{1,0:T(8,128)(2,1)}) %all-gather.3.cloned.1.call-update) | async-done | bytes 8388624 | tf_op jit(solution)/shard_map/all_gather | solution.py:510
  163.0 21.2 %down_pass.1 = (bf16[8,4,256,1024]{3,2,1,0:T(8,128)(2,1)}, f32[2048,1024]{1,0:T(8,128)}) custom-call(bf16[4096,1024]{1,0:T(8,128)(2,1)} %all-gather.3.cloned.1.call-done.v_ref, bf16[8,2,512,256]{3,2,1,0:T(8,128)(2,1)} %fusion.p_ref, bf16[2048,2048]{1,0:T(8,128)(2,1)} %get-tuple-element.14.w_ref), custom_call_target="tpu_custom_call" | custom-call | flops 12884901888 | bytes 46137344 | tf_op jit(solution)/shard_map/down_pass/pallas_call | solution.py:193
  184.2 4.1 %fusion.7 = (f32[512,1024]{1,0:T(8,128)}, f32[512,1024]{1,0:T(8,128)S(1)}) fusion(f32[2048,1024]{1,0:T(8,128)} %get-tuple-element.15), kind=kLoop, calls=%fused_computation.34 | loop fusion | bytes 8388608 | tf_op jit(solution)/shard_map/slice | solution.py:522
  188.3 0.4 collective-permute-start.12
  188.7 3.8 %collective-permute-done.12 = f32[512,1024]{1,0:T(8,128)S(1)} collective-permute-done((f32[512,1024]{1,0:T(8,128)S(1)}, f32[512,1024]{1,0:T(8,128)S(1)}, u32[]{:S(2)}, u32[]{:S(2)}) %collective-permute-start.12) | collective-permute-done | bytes 2097184 | tf_op jit(solution)/shard_map/ppermute | solution.py:498
  192.5 2.0 slice_add_fusion.2
  194.5 38.9 %second_pass.1 = (bf16[2048,2048]{1,0:T(8,128)(2,1)}, bf16[4096,1024]{1,0:T(8,128)(2,1)}) custom-call(bf16[8,4,256,1024]{3,2,1,0:T(8,128)(2,1)} %get-tuple-element.18.vc_ref, bf16[8,4,2,256,128]{4,3,2,1,0:T(8,128)(2,1)} %fusion.1.pt_ref, f32[2048,2048]{1,0:T(8,128)} %get-tuple-element.19.s_ref, bf16[512,1024]{1,0:T(8,128)(2,1)} %refs_0_.1, ...), custom_call_target="tpu_custom_call" | custom-call | flops 27917287424 | bytes 60817408 | tf_op jit(solution)/shard_map/second_pass/pallas_call | solution.py:244
  233.4 8.9 %token_grad.3 = f32[1024,1024]{1,0:T(8,128)} custom-call(bf16[2048,2048]{1,0:T(8,128)(2,1)} %get-tuple-element.20.c_ref, bf16[8,4,256,1024]{3,2,1,0:T(8,128)(2,1)} %get-tuple-element.21.uc_ref), custom_call_target="tpu_custom_call" | custom-call | flops 4294967296 | bytes 16777216 | tf_op jit(solution)/shard_map/token_grad/pallas_call | solution.py:276
  242.3 3.3 slice.64
  245.6 0.1 collective-permute-start.15
  245.7 0.4 collective-permute-start.11
  246.1 1.3 collective-permute-start.13
  247.4 9.0 %token_grad.2 = f32[1024,1024]{1,0:T(8,128)} custom-call(bf16[2048,2048]{1,0:T(8,128)(2,1)} %get-tuple-element.20.c_ref, bf16[8,4,256,1024]{3,2,1,0:T(8,128)(2,1)} %get-tuple-element.21.uc_ref), custom_call_target="tpu_custom_call" | custom-call | flops 4294967296 | bytes 16777216 | tf_op jit(solution)/shard_map/token_grad/pallas_call | solution.py:276
  256.3 3.4 slice.62
  259.7 0.3 collective-permute-start.14
  260.1 3.3 slice_add_fusion
  263.4 0.3 collective-permute-start.16
  263.7 57.5 %reduce_rows.1 = bf16[128,1024]{1,0:T(8,128)(2,1)S(1)} custom-call(bf16[4096,1024]{1,0:T(8,128)(2,1)} %get-tuple-element.22.part_ref), custom_call_target="tpu_custom_call" | custom-call | flops 1000000000 | bytes 16777216 | tf_op jit(solution)/shard_map/reduce_rows/pallas_call | solution.py:466
  321.2 4.4 %add_convert_fusion = bf16[512,1024]{1,0:T(8,128)(2,1)} fusion(f32[512,1024]{1,0:T(8,128)} %collective-permute-done.13, f32[512,1024]{1,0:T(8,128)} %collective-permute-done.11, f32[2048,1024]{1,0:T(8,128)} %get-tuple-element.15), kind=kLoop, calls=%fused_computation.12 | loop fusion | flops 1572864 | bytes 7340032 | tf_op jit(solution)/shard_map/convert_element_type | solution.py:523
  325.6 1.0 constant_dynamic-slice_fusion
  326.5 1.9 collective-permute-start.17
  328.4 9.7 %collective-permute-done.16 = f32[512,1024]{1,0:T(8,128)} collective-permute-done((f32[512,1024]{1,0:T(8,128)}, f32[512,1024]{1,0:T(8,128)}, u32[]{:S(2)}, u32[]{:S(2)}) %collective-permute-start.16) | collective-permute-done | bytes 2097184 | tf_op jit(solution)/shard_map/ppermute | solution.py:498
  338.2 4.4 %fusion.3 = bf16[512,1024]{1,0:T(8,128)(2,1)} fusion(f32[512,1024]{1,0:T(8,128)} %collective-permute-done.16, f32[512,1024]{1,0:T(8,128)} %collective-permute-done.14, f32[1024,1024]{1,0:T(8,128)} %token_grad.2), kind=kLoop, calls=%fused_computation.11 | loop fusion | flops 1572864 | bytes 7340032 | tf_op jit(solution)/shard_map/convert_element_type | solution.py:523
  342.6 0.8 add_convert_fusion.1
  343.3 0.7 copy.26
  (54 shorter events, 0.3 us)
Async XLA Ops:
  7.2 22.4 %copy-start.5 = (s32[1,128,64]{1,2,0:T(8,128)S(1)}, s32[1,128,64]{1,2,0:T(8,128)}, u32[]{:S(2)}) copy-start(s32[1,128,64]{1,2,0:T(8,128)} %param.11) | copy-start | bytes 98308
  7.2 22.6 %copy-start.3 = (s32[512,4,32]{0,2,1:T(8,128)S(1)}, s32[512,4,32]{0,2,1:T(8,128)}, u32[]{:S(2)}) copy-start(s32[512,4,32]{0,2,1:T(8,128)} %param.10) | copy-start | bytes 786436
  7.2 99.7 %all-gather.5.cloned.1.call-start = ((), (), s32[]{:S(2)}) async-start(), calls=%async_computation.2 | async-start | bytes 8912896 | tf_op jit(solution)/shard_map/all_gather | solution.py:510
  7.2 10.1 %collective-permute-start.4 = (bf16[128,1024]{1,0:T(8,128)(2,1)}, bf16[128,1024]{1,0:T(8,128)(2,1)S(1)}, u32[]{:S(2)}, u32[]{:S(2)}) collective-permute-start(bf16[128,1024]{1,0:T(8,128)(2,1)} %param.14), channel_id=1, source_target_pairs={{0,96},{1,97},{2,98},{3,99},{4,100},{5,101},{6,102},{7,103},{8,104... | collective-permute-start | bytes 786440 | tf_op jit(solution)/shard_map/ppermute | solution.py:498
  11.1 18.9 %copy-start.4 = (f32[512,4,32]{0,2,1:T(8,128)S(1)}, f32[512,4,32]{0,2,1:T(8,128)}, u32[]{:S(2)}) copy-start(f32[512,4,32]{0,2,1:T(8,128)} %param.12) | copy-start | bytes 786436
  19.3 13.1 %copy-start.9 = (bf16[512,1024]{1,0:T(8,128)(2,1)S(1)}, bf16[512,1024]{1,0:T(8,128)(2,1)}, u32[]{:S(2)}) copy-start(bf16[512,1024]{1,0:T(8,128)(2,1)} %refs_0_.1) | copy-start | bytes 3145732
  19.3 143.7 %all-gather.3.cloned.1.call-start = ((), (), s32[]{:S(2)}) async-start(), calls=%async_computation.1 | async-start | bytes 8912896 | tf_op jit(solution)/shard_map/all_gather | solution.py:510
  19.4 8.1 %collective-permute-start = (bf16[128,1024]{1,0:T(8,128)(2,1)}, bf16[128,1024]{1,0:T(8,128)(2,1)S(1)}, u32[]{:S(2)}, u32[]{:S(2)}) collective-permute-start(bf16[128,1024]{1,0:T(8,128)(2,1)} %param.15), channel_id=1, source_target_pairs={{0,96},{1,97},{2,98},{3,99},{4,100},{5,101},{6,102},{7,103},{8,104... | collective-permute-start | bytes 786440 | tf_op jit(solution)/shard_map/ppermute | solution.py:498
  29.5 5.4 %copy-start.10 = (s32[2]{0:T(128)S(1)}, s32[2]{0:T(128)}, u32[]{:S(2)}) copy-start(s32[2]{0:T(128)} %constant.70.clone) | copy-start | bytes 28
  29.5 296.0 %reduce-scatter.2.cloned.1.call-start = ((), (), s32[]{:S(2)}) async-start(), calls=%async_computation.3 | async-start | bytes 8912896 | tf_op jit(solution)/shard_map/reduce_scatter | solution.py:513
  30.1 4.8 %copy-start.1 = (f32[1088,128]{1,0:T(8,128)}, f32[1088,128]{1,0:T(8,128)S(1)}, u32[]{:S(2)}) copy-start(f32[1088,128]{1,0:T(8,128)S(1)} %pad_maximum_fusion.slot_ref.gate_ref) | copy-start | bytes 1671172
  30.1 15.4 %collective-permute-start.2 = (f32[1088,128]{1,0:T(8,128)S(1)}, f32[1088,128]{1,0:T(8,128)S(1)}, u32[]{:S(2)}, u32[]{:S(2)}) collective-permute-start(f32[1088,128]{1,0:T(8,128)S(1)} %pad_maximum_fusion.slot_ref.gate_ref), channel_id=1, source_target_pairs={{0,32},{1,33},{2,34},{3,35},{4,36},{5,37},{6,38},{7,39},{8,40},{9,... | collective-permute-start | bytes 1671176 | tf_op jit(solution)/shard_map/ppermute | solution.py:498
  30.2 14.0 %collective-permute-start.1 = (f32[1088,128]{1,0:T(8,128)S(1)}, f32[1088,128]{1,0:T(8,128)S(1)}, u32[]{:S(2)}, u32[]{:S(2)}) collective-permute-start(f32[1088,128]{1,0:T(8,128)S(1)} %pad_maximum_fusion.slot_ref.gate_ref), channel_id=1, source_target_pairs={{0,1},{1,0},{2,3},{3,2},{4,5},{5,4},{6,7},{7,6},{8,9},{9,8},{10,11... | collective-permute-start | bytes 1671176 | tf_op jit(solution)/shard_map/ppermute | solution.py:498
  32.4 57.9 %collective-permute-start.6 = (bf16[512,1024]{1,0:T(8,128)(2,1)S(1)}, bf16[512,1024]{1,0:T(8,128)(2,1)}, u32[]{:S(2)}, u32[]{:S(2)}) collective-permute-start(bf16[512,1024]{1,0:T(8,128)(2,1)S(1)} %copy-done.9), channel_id=1, source_target_pairs={{0,32},{1,33},{2,34},{3,35},{4,36},{5,37},{6,38},{7,39},{8,40},{9,... | collective-permute-start | bytes 3145736 | tf_op jit(solution)/shard_map/ppermute | solution.py:498
  34.1 72.7 %collective-permute-start.5 = (bf16[512,1024]{1,0:T(8,128)(2,1)S(1)}, bf16[512,1024]{1,0:T(8,128)(2,1)}, u32[]{:S(2)}, u32[]{:S(2)}) collective-permute-start(bf16[512,1024]{1,0:T(8,128)(2,1)S(1)} %copy-done.9), channel_id=1, source_target_pairs={{0,1},{1,0},{2,3},{3,2},{4,5},{5,4},{6,7},{7,6},{8,9},{9,8},{10,11... | collective-permute-start | bytes 3145736 | tf_op jit(solution)/shard_map/ppermute | solution.py:498
  34.3 53.0 %collective-permute-start.9 = (bf16[512,1024]{1,0:T(8,128)(2,1)}, bf16[512,1024]{1,0:T(8,128)(2,1)}, u32[]{:S(2)}, u32[]{:S(2)}) collective-permute-start(bf16[512,1024]{1,0:T(8,128)(2,1)} %refs_4_.3), channel_id=1, source_target_pairs={{0,32},{1,33},{2,34},{3,35},{4,36},{5,37},{6,38},{7,39},{8,40},{9,... | collective-permute-start | bytes 3145736 | tf_op jit(solution)/shard_map/ppermute | solution.py:498
  44.3 4.3 %copy-start.7 = (f32[1088,128]{1,0:T(8,128)}, f32[1088,128]{1,0:T(8,128)S(1)}, u32[]{:S(2)}) copy-start(f32[1088,128]{1,0:T(8,128)S(1)} %collective-permute-done.1.slot_ref.gate_ref) | copy-start | bytes 1671172
  44.3 62.5 %collective-permute-start.8 = (bf16[512,1024]{1,0:T(8,128)(2,1)}, bf16[512,1024]{1,0:T(8,128)(2,1)}, u32[]{:S(2)}, u32[]{:S(2)}) collective-permute-start(bf16[512,1024]{1,0:T(8,128)(2,1)} %refs_4_.3), channel_id=1, source_target_pairs={{0,1},{1,0},{2,3},{3,2},{4,5},{5,4},{6,7},{7,6},{8,9},{9,8},{10,11... | collective-permute-start | bytes 3145736 | tf_op jit(solution)/shard_map/ppermute | solution.py:498
  45.5 11.7 %copy-start.6 = (f32[1088,128]{1,0:T(8,128)}, f32[1088,128]{1,0:T(8,128)S(1)}, u32[]{:S(2)}) copy-start(f32[1088,128]{1,0:T(8,128)S(1)} %collective-permute-done.2.slot_ref.gate_ref) | copy-start | bytes 1671172
  46.2 44.1 %collective-permute-start.3 = (f32[1088,128]{1,0:T(8,128)S(1)}, f32[1088,128]{1,0:T(8,128)S(1)}, u32[]{:S(2)}, u32[]{:S(2)}) collective-permute-start(f32[1088,128]{1,0:T(8,128)S(1)} %collective-permute-done.2.slot_ref.gate_ref), channel_id=1, source_target_pairs={{0,1},{1,0},{2,3},{3,2},{4,5},{5,4},{6,7},{7,6},{8,9},{9,8},{10,11... | collective-permute-start | bytes 1671176 | tf_op jit(solution)/shard_map/ppermute | solution.py:498
  87.3 19.5 %collective-permute-start.10 = (bf16[512,1024]{1,0:T(8,128)(2,1)}, bf16[512,1024]{1,0:T(8,128)(2,1)}, u32[]{:S(2)}, u32[]{:S(2)}) collective-permute-start(bf16[512,1024]{1,0:T(8,128)(2,1)} %collective-permute-done.9.refs_10_.refs_6_), channel_id=1, source_target_pairs={{0,1},{1,0},{2,3},{3,2},{4,5},{5,4},{6,7},{7,6},{8,9},{9,8},{10,11... | collective-permute-start | bytes 3145736 | tf_op jit(solution)/shard_map/ppermute | solution.py:498
  90.3 16.5 %collective-permute-start.7 = (bf16[512,1024]{1,0:T(8,128)(2,1)}, bf16[512,1024]{1,0:T(8,128)(2,1)}, u32[]{:S(2)}, u32[]{:S(2)}) collective-permute-start(bf16[512,1024]{1,0:T(8,128)(2,1)} %collective-permute-done.6.refs_6_.refs_2_), channel_id=1, source_target_pairs={{0,1},{1,0},{2,3},{3,2},{4,5},{5,4},{6,7},{7,6},{8,9},{9,8},{10,11... | collective-permute-start | bytes 3145736 | tf_op jit(solution)/shard_map/ppermute | solution.py:498
  90.3 4.2 %copy-start.8 = (f32[1088,128]{1,0:T(8,128)}, f32[1088,128]{1,0:T(8,128)S(1)}, u32[]{:S(2)}) copy-start(f32[1088,128]{1,0:T(8,128)S(1)} %collective-permute-done.3.slot_ref.gate_ref) | copy-start | bytes 1671172
  188.3 4.2 %collective-permute-start.12 = (f32[512,1024]{1,0:T(8,128)S(1)}, f32[512,1024]{1,0:T(8,128)S(1)}, u32[]{:S(2)}, u32[]{:S(2)}) collective-permute-start(f32[512,1024]{1,0:T(8,128)S(1)} %get-tuple-element.25), channel_id=1, source_target_pairs={{0,1},{1,0},{2,3},{3,2},{4,5},{5,4},{6,7},{7,6},{8,9},{9,8},{10,11... | collective-permute-start | bytes 6291464 | tf_op jit(solution)/shard_map/ppermute | solution.py:498
  245.6 14.5 %collective-permute-start.15 = (f32[512,1024]{1,0:T(8,128)}, f32[512,1024]{1,0:T(8,128)}, u32[]{:S(2)}, u32[]{:S(2)}) collective-permute-start(f32[512,1024]{1,0:T(8,128)} %slice.64), channel_id=1, source_target_pairs={{0,1},{1,0},{2,3},{3,2},{4,5},{5,4},{6,7},{7,6},{8,9},{9,8},{10,11... | collective-permute-start | bytes 6291464 | tf_op jit(solution)/shard_map/ppermute | solution.py:498
  245.7 75.4 %collective-permute-start.11 = (f32[512,1024]{1,0:T(8,128)}, f32[512,1024]{1,0:T(8,128)}, u32[]{:S(2)}, u32[]{:S(2)}) collective-permute-start(f32[512,1024]{1,0:T(8,128)} %get-tuple-element.24), channel_id=1, source_target_pairs={{0,1},{1,0},{2,3},{3,2},{4,5},{5,4},{6,7},{7,6},{8,9},{9,8},{10,11... | collective-permute-start | bytes 6291464 | tf_op jit(solution)/shard_map/ppermute | solution.py:498
  246.1 75.1 %collective-permute-start.13 = (f32[512,1024]{1,0:T(8,128)S(1)}, f32[512,1024]{1,0:T(8,128)}, u32[]{:S(2)}, u32[]{:S(2)}) collective-permute-start(f32[512,1024]{1,0:T(8,128)S(1)} %slice_add_fusion.2), channel_id=1, source_target_pairs={{0,32},{1,33},{2,34},{3,35},{4,36},{5,37},{6,38},{7,39},{8,40},{9,... | collective-permute-start | bytes 6291464 | tf_op jit(solution)/shard_map/ppermute | solution.py:498
  256.3 3.7 %copy-start = (f32[1024,1024]{1,0:T(8,128)S(1)}, f32[1024,1024]{1,0:T(8,128)}, u32[]{:S(2)}) copy-start(f32[1024,1024]{1,0:T(8,128)} %token_grad.3) | copy-start | bytes 12582916
  259.7 68.7 %collective-permute-start.14 = (f32[512,1024]{1,0:T(8,128)}, f32[512,1024]{1,0:T(8,128)}, u32[]{:S(2)}, u32[]{:S(2)}) collective-permute-start(f32[512,1024]{1,0:T(8,128)} %slice.62), channel_id=1, source_target_pairs={{0,1},{1,0},{2,3},{3,2},{4,5},{5,4},{6,7},{7,6},{8,9},{9,8},{10,11... | collective-permute-start | bytes 6291464 | tf_op jit(solution)/shard_map/ppermute | solution.py:498
  263.4 74.8 %collective-permute-start.16 = (f32[512,1024]{1,0:T(8,128)}, f32[512,1024]{1,0:T(8,128)}, u32[]{:S(2)}, u32[]{:S(2)}) collective-permute-start(f32[512,1024]{1,0:T(8,128)} %slice_add_fusion), channel_id=1, source_target_pairs={{0,32},{1,33},{2,34},{3,35},{4,36},{5,37},{6,38},{7,39},{8,40},{9,... | collective-permute-start | bytes 6291464 | tf_op jit(solution)/shard_map/ppermute | solution.py:498
  326.5 16.0 %copy-start.2 = (bf16[256,1024]{1,0:T(8,128)(2,1)S(1)}, bf16[256,1024]{1,0:T(8,128)(2,1)}, u32[]{:S(2)}) copy-start(bf16[256,1024]{1,0:T(8,128)(2,1)} %reduce-scatter.2.cloned.1.call-done) | copy-start | bytes 1572868
  326.5 16.0 %collective-permute-start.17 = (bf16[128,1024]{1,0:T(8,128)(2,1)S(1)}, bf16[128,1024]{1,0:T(8,128)(2,1)S(1)}, u32[]{:S(2)}, u32[]{:S(2)}) collective-permute-start(bf16[128,1024]{1,0:T(8,128)(2,1)S(1)} %constant_dynamic-slice_fusion), channel_id=1, source_target_pairs={{0,96},{1,97},{2,98},{3,99},{4,100},{5,101},{6,102},{7,103},{8,104... | collective-permute-start | bytes 786440 | tf_op jit(solution)/shard_map/ppermute | solution.py:498
Sparse Core Ops, SparseCore 0:
  19.4 71.0 all-gather.4
  92.6 70.3 all-gather.2
  166.4 83.9 reduce-scatter.1
where the time goes:
time: 354 us; the launch traced here: 351 us
  Pallas kernels  221 us (62%)
  waiting for transfers between devices  51.9 us (15%)
  other arithmetic  26.6 us (8%)
  starting transfers between devices  21.2 us (6%)
  local copies, waits for them, and re-layouts  15.6 us (4%)
  between operations  14 us (4%)
    pallas_call x1, Pallas kernels, reduce_rows(): pl.pallas_call(reduce_kernel, in_specs=[vmem], out_specs=vmem, out_shape=...  57.5 us
    pallas_call x1, Pallas kernels, first_pass(): pl.pallas_call(functools.partial(first_kernel, n_tok), grid=(N_GRP,), in_...  51.3 us
    ppermute x18, waiting for transfers between devices, swap(): return lax.ppermute(arr, 'ep', [(i, i ^ mask) for i in range(N_EP)])  46.9 us
    pallas_call x1, Pallas kernels, second_pass(): pl.pallas_call(functools.partial(second_kernel, n_tok), grid=(N_GRP,), in...  38.9 us
    pallas_call x4, Pallas kernels, gate_matrix(): pl.pallas_call(gate_kernel, grid=(n_blk,), in_specs=[pl.BlockSpec(memory_...  34.5 us
    pallas_call x1, Pallas kernels, down_pass(): pl.pallas_call(functools.partial(down_kernel, n_tok), grid=(N_GRP,), in_s...  21.2 us
    ppermute x18, starting transfers between devices, swap(): return lax.ppermute(arr, 'ep', [(i, i ^ mask) for i in range(N_EP)])  21.1 us
    pallas_call x2, Pallas kernels, token_grad(): pl.pallas_call(token_grad_kernel, grid=(2,), in_specs=[pl.BlockSpec((n_to...  17.9 us
  transfers between devices with their start and end apart: 21, of which 6 were waited for; matrix products, arithmetic and copies ran while one was open for 11% of the time, Pallas kernels for 63%

commit v1 on v0

--- a/solution.py
+++ b/solution.py
@@ -33,8 +33,9 @@
     slot = slot_ref[...].astype(jnp.int32)
     owner = slot >> 6
     z_of = owner >> 5
-    here = ((owner & 1) == ctl_ref[0]) & ((((z_of + 1) >> 1) & 1) == ctl_ref[1])
-    local = ((((owner >> 1) & 15) * 2 + (z_of >> 1)) << 6) + (slot & 63)
+    same_plane = z_of == ctl_ref[1]
+    here = ((owner & 1) == ctl_ref[0]) & (same_plane | (z_of == 3 - ctl_ref[1]))
+    local = ((((owner >> 1) & 15) * 2 + jnp.where(same_plane, 0, 1)) << 6) + (slot & 63)
     hi_ref[...] = jnp.where(here, local >> 7, 255).astype(F32)
     lo_ref[...] = (local & 127).astype(F32)
     gate = gate_ref[...]
@@ -175,14 +176,15 @@
     )(u_all, p_hot, pt_hot, *gates, *xs, *dys)
 
 
-def down_kernel(n_tok, v_ref, p_ref, w_ref, vc_ref, y_ref):
+def down_kernel(n_tok, v_ref, p_ref, w_ref, vc_ref, *y_refs):
     @pl.when(pl.program_id(0) == 0)
     def _():
-        y_ref[...] = jnp.zeros_like(y_ref)
+        for y_ref in y_refs:
+            y_ref[...] = jnp.zeros_like(y_ref)
 
     pick_rows(p_ref, v_ref, vc_ref)
     for s in range(N_SET):
-        y_ref[s * n_tok:(s + 1) * n_tok, :] += dot(w_ref[s * n_tok:(s + 1) * n_tok, :], vc_ref[0, s])
+        y_refs[s][...] += dot(w_ref[s * n_tok:(s + 1) * n_tok, :], vc_ref[0, s])
 
 
 def down_pass(v_all, p_hot, w_all):
@@ -200,12 +202,10 @@
         ],
         out_specs=[
             pl.BlockSpec((1, N_SET, 256, width), lambda g: (g, 0, 0, 0)),
-            pl.BlockSpec((all_tok, width), lambda g: (0, 0)),
-        ],
+        ] + [pl.BlockSpec((n_tok, width), lambda g: (0, 0))] * N_SET,
         out_shape=[
             jax.ShapeDtypeStruct((N_GRP, N_SET, 256, width), BF16),
-            jax.ShapeDtypeStruct((all_tok, width), F32),
-        ],
+        ] + [jax.ShapeDtypeStruct((n_tok, width), F32)] * N_SET,
         compiler_params=pltpu.CompilerParams(vmem_limit_bytes=60 * 2 ** 20),
         cost_estimate=pl.CostEstimate(flops=flops, bytes_accessed=44 * 2 ** 20, transcendentals=0),
         name="down_pass",
@@ -264,30 +264,6 @@
     )(vc, pt_hot, slopes, *xs, *dys)
 
 
-def token_grad_kernel(c_ref, uc_ref, dx_ref):
-    width = uc_ref.shape[-1]
-    dx_ref[...] = dot(c_ref[...], uc_ref[...].reshape(N_GRP * 256, width))
-
-
-def token_grad(c_all, uc, first_set):
-    width = uc.shape[-1]
-    n_tok = c_all.shape[0] // N_SET
-    flops = 2 * 2 * n_tok * N_GRP * 256 * width
-    return pl.pallas_call(
-        token_grad_kernel,
-        grid=(2,),
-        in_specs=[
-            pl.BlockSpec((n_tok, N_GRP * 256), lambda i: (first_set + i, 0)),
-            pl.BlockSpec((N_GRP, 1, 256, width), lambda i: (0, first_set + i, 0, 0)),
-        ],
-        out_specs=pl.BlockSpec((n_tok, width), lambda i: (i, 0)),
-        out_shape=jax.ShapeDtypeStruct((2 * n_tok, width), F32),
-        compiler_params=pltpu.CompilerParams(vmem_limit_bytes=60 * 2 ** 20),
-        cost_estimate=pl.CostEstimate(flops=flops, bytes_accessed=16 * 2 ** 20, transcendentals=0),
-        name="token_grad",
-    )(c_all, uc)
-
-
 def ring_place():
     me = lax.axis_index('ep')
     core, x_me, y_me, z_me = me % 2, (me // 2) % 4, (me // 8) % 4, me // 32
@@ -305,26 +281,43 @@
     pl.semaphore_wait(barrier, len(peers))
 
 
-HALF_A, HALF_B, N_MSG = (2, 1), (3, 0), 19
-
-
-def reduce_kernel(part_ref, out_ref, s1_prev, s1_next, s2_prev, s2_next, sum_next, sum_prev, mid, t1_prev, t1_next, t2_prev, t2_next, tsum_next, tsum_prev, keep, z_send, z_recv, send_sem, recv_sem):
+HALF_A, HALF_B, N_MSG, N_TILE = (2, 1), (3, 0), 19, 4
+
+
+def tail_kernel(part_ref, c_ref, uc_ref, y0_ref, yc_ref, yz_ref, out_ref, dx_ref, y_ref,
+                own_next, own_prev, own_mid, s1_prev, s1_next, s2_prev, s2_next, sum_next, sum_prev, mid,
+                t1_prev, t1_next, t2_prev, t2_next, tsum_next, tsum_prev, keep, z_send, z_recv,
+                c_buf, uc_buf, dx_part, core_recv, far_send, far_recv, y_in,
+                send_sem, recv_sem, own_sem, load_sem, y_sem, core_send_sem, core_recv_sem, far_send_sem, far_recv_sem):
     rows, width = out_ref.shape
     half = width // 2
+    n_tok = dx_ref.shape[0]
+    tile = n_tok // N_TILE
     x_me, y_me, z_me, device = ring_place()
+    me = lax.axis_index('ep')
     z_peer = device(3 - z_me, y_me, x_me)
-    upper = z_me // 2
+    core_peer = me + 1 - 2 * (me % 2)
+    far_peer = device(z_me + 1 - 2 * (z_me % 2), y_me, x_me)
     x_next, x_prev = device(z_me, y_me, (x_me + 1) % 4), device(z_me, y_me, (x_me + 3) % 4)
     y_next, y_prev = device(z_me, (y_me + 1) % 4, x_me), device(z_me, (y_me + 3) % 4, x_me)
-    meet((x_next, x_prev, y_next, y_prev, z_peer))
     chunk = 32
 
-    def add_up(n_rows, store, *loads):
+    def load_set(s, slot):
+        return (pltpu.make_async_copy(c_ref.at[pl.ds(s * n_tok, n_tok)], c_buf.at[slot], load_sem.at[s, 0]),
+                pltpu.make_async_copy(uc_ref.at[:, s], uc_buf.at[slot], load_sem.at[s, 1]))
+
+    loads = {s: load_set(s, s % 2) for s in range(N_SET)}
+    for s in (3, 2):
+        for copy in loads[s]:
+            copy.start()
+    meet((x_next, x_prev, y_next, y_prev, z_peer, core_peer, far_peer))
+
+    def add_up(n_rows, store, *parts):
         def step(i, carry):
             at = pl.ds(pl.multiple_of(i * chunk, chunk), chunk)
-            total = loads[0](i, at)
-            for load in loads[1:]:
-                total = total + load(i, at)
+            total = parts[0](i, at)
+            for one_part in parts[1:]:
+                total = total + one_part(i, at)
             store(at, total)
             return carry
 
@@ -346,29 +339,24 @@
     for k in range(2):
         one = Side()
         one.k = k
-        first, second = (x_me, y_me) if k == 0 else (y_me, x_me)
-        one.first, one.second = first, second
+        one.first, one.second = (x_me, y_me) if k == 0 else (y_me, x_me)
         one.next1, one.prev1 = (x_next, x_prev) if k == 0 else (y_next, y_prev)
         one.next2, one.prev2 = (y_next, y_prev) if k == 0 else (x_next, x_prev)
         sides.append(one)
 
-    def start_of(one, shift1, shift2):
+    def own(one, shift1, shift2):
         first, second = (one.first + shift1) % 4, (one.second + shift2) % 4
         chip = second * 4 + first if one.k == 0 else first * 4 + second
-        return chip * (2 * rows)
-
-    def own(one, shift1, shift2):
-        return part_ref.at[pl.ds(pl.multiple_of(start_of(one, shift1, shift2), 2 * rows), 2 * rows), pl.ds(one.k * half, half)]
-
-    def load_own(one, shift1, shift2):
-        start = start_of(one, shift1, shift2)
-        return lambda i, at: part_ref[pl.ds(pl.multiple_of(start + i * chunk, chunk), chunk), one.k * half:(one.k + 1) * half].astype(F32)
+        return part_ref.at[pl.ds(pl.multiple_of(chip * (2 * rows), 2 * rows), 2 * rows), pl.ds(one.k * half, half)]
+
+    def remote(src, dst, sems, peer):
+        return pltpu.make_async_remote_copy(src_ref=src, dst_ref=dst, send_sem=sems[0], recv_sem=sems[1],
+                                            device_id={'ep': peer}, device_id_type=pl.DeviceIdType.MESH)
 
     def message(one, number, src, dst, peer):
-        return pltpu.make_async_remote_copy(
-            src_ref=src, dst_ref=dst, send_sem=send_sem.at[one.k, number], recv_sem=recv_sem.at[one.k, number],
-            device_id={'ep': peer}, device_id_type=pl.DeviceIdType.MESH)
-
+        return remote(src, dst, (send_sem.at[one.k, number], recv_sem.at[one.k, number]), peer)
+
+    lower_rows, upper_rows = pl.ds(0, rows), pl.ds(rows, rows)
     for one in sides:
         k = one.k
         one.s1n = [message(one, i, own(one, 2, HALF_A[i]), s1_prev.at[k, i], one.next1) for i in range(2)]
@@ -377,7 +365,6 @@
         one.inp = [message(one, 6 + i, own(one, 3, HALF_A[i]), s2_next.at[k, HALF_A[i]], one.prev1) for i in range(2)]
         one.dpn = [message(one, 8 + i, sum_next.at[k, i], s2_prev.at[k, HALF_A[i]], one.next1) for i in range(2)]
         one.dpp = [message(one, 10 + i, sum_prev.at[k, i], s2_next.at[k, HALF_B[i]], one.prev1) for i in range(2)]
-        lower_rows, upper_rows = pl.ds(0, rows), pl.ds(rows, rows)
         one.t1n = message(one, 12, mid.at[k, 2, lower_rows], t1_prev.at[k], one.next2)
         one.t1p = message(one, 13, mid.at[k, 2, upper_rows], t1_next.at[k], one.prev2)
         one.tin = message(one, 14, mid.at[k, 1, upper_rows], t2_prev.at[k, 1], one.next2)
@@ -385,6 +372,24 @@
         one.tdn = message(one, 16, tsum_next.at[k], t2_prev.at[k, 0], one.next2)
         one.tdp = message(one, 17, tsum_prev.at[k], t2_next.at[k, 1], one.prev2)
         one.zz = message(one, 18, z_send.at[k], z_recv.at[k], z_peer)
+        one.stage = [pltpu.make_async_copy(own(one, 1, HALF_A[i]), own_next.at[k, i], own_sem.at[k, i]) for i in range(2)]
+        one.stage += [pltpu.make_async_copy(own(one, 3, HALF_B[i]), own_prev.at[k, i], own_sem.at[k, 2 + i]) for i in range(2)]
+        one.stage += [pltpu.make_async_copy(own(one, 0, r), own_mid.at[k, r], own_sem.at[k, 4 + r]) for r in range(4)]
+
+    def core_msg(which, t):
+        at = pl.ds(pl.multiple_of(t * tile, tile), tile)
+        return remote(dx_part.at[3 - 2 * which, at], core_recv.at[which, at], (core_send_sem.at[which, t], core_recv_sem.at[which, t]), core_peer)
+
+    def far_msg(t):
+        at = pl.ds(pl.multiple_of(t * tile, tile), tile)
+        return remote(far_send.at[at], far_recv.at[at], (far_send_sem.at[t], far_recv_sem.at[t]), far_peer)
+
+    def tiles(body):
+        lax.fori_loop(0, N_TILE, lambda t, carry: (body(t), carry)[1], 0)
+
+    def dx_tile(s, t):
+        at = pl.ds(pl.multiple_of(t * tile, tile), tile)
+        dx_part[s, at, :] = dot(c_buf[s % 2, at, :], uc_buf[s % 2].reshape(N_GRP * 256, width))
 
     for i in range(2):
         for one in sides:
@@ -394,14 +399,71 @@
         for one in sides:
             one.inn[i].start()
             one.inp[i].start()
+    for one in sides:
+        for copy in one.stage:
+            copy.start()
+    y_loads = [pltpu.make_async_copy(src, y_in.at[i], y_sem.at[i]) for i, src in enumerate((y0_ref, yc_ref, yz_ref))]
+    for copy in y_loads:
+        copy.start()
+
+    for s in (3, 2):
+        for copy in loads[s]:
+            copy.wait()
+
+    def far_tile(t):
+        dx_tile(3, t)
+        core_msg(0, t).start()
+        dx_tile(2, t)
+
+    tiles(far_tile)
+    for s in (1, 0):
+        for copy in loads[s]:
+            copy.start()
+
+    def far_sum(t):
+        core_msg(0, t).wait_recv()
+
+        def step(i, carry):
+            at = pl.ds(pl.multiple_of(t * tile + i * 32, 32), 32)
+            far_send[at, :] = dx_part[2, at, :] + core_recv[0, at, :]
+            return carry
+
+        lax.fori_loop(0, tile // 32, step, 0)
+        far_msg(t).start()
+
+    tiles(far_sum)
+
+    for one in sides:
+        for copy in one.stage:
+            copy.wait()
     for i in range(2):
         for one in sides:
+            k = one.k
             one.s1n[i].wait_recv()
-            add_up(2 * rows, into_buf(sum_next, one.k, i), load_own(one, 1, HALF_A[i]), from_buf(s1_prev, one.k, i))
+            add_up(2 * rows, into_buf(sum_next, k, i), from_buf(own_next, k, i), from_buf(s1_prev, k, i))
             one.dpn[i].start()
             one.s1p[i].wait_recv()
-            add_up(2 * rows, into_buf(sum_prev, one.k, i), load_own(one, 3, HALF_B[i]), from_buf(s1_next, one.k, i))
+            add_up(2 * rows, into_buf(sum_prev, k, i), from_buf(own_prev, k, i), from_buf(s1_next, k, i))
             one.dpp[i].start()
+
+    for s in (1, 0):
+        for copy in loads[s]:
+            copy.wait()
+
+    def near_tile(t):
+        dx_tile(1, t)
+        core_msg(1, t).start()
+        dx_tile(0, t)
+
+    tiles(near_tile)
+    for copy in y_loads:
+        copy.wait()
+
+    def y_store(at, total):
+        y_ref[at, :] = total.astype(BF16)
+
+    add_up(n_tok, y_store, from_buf(y_in, 0), from_buf(y_in, 1), from_buf(y_in, 2))
+
     for i, r in ((0, 2), (0, 3), (1, 1), (1, 0)):
         for one in sides:
             k = one.k
@@ -411,7 +473,7 @@
             else:
                 one.inn[i].wait_recv()
                 one.dpp[i].wait_recv()
-            add_up(2 * rows, into_buf(mid, k, r), load_own(one, 0, r), from_buf(s2_prev, k, r), from_buf(s2_next, k, r))
+            add_up(2 * rows, into_buf(mid, k, r), from_buf(own_mid, k, r), from_buf(s2_prev, k, r), from_buf(s2_next, k, r))
             if r == 2:
                 one.t1n.start()
                 one.t1p.start()
@@ -433,17 +495,9 @@
         one.tip.wait_recv()
         one.tdn.wait_recv()
         one.tdp.wait_recv()
-
-        def last_sum(i, carry, k=k):
-            at = pl.ds(pl.multiple_of(i * chunk, chunk), chunk)
-            low = mid[k, 0, at, :].astype(F32) + t2_prev[k, 0, at, :].astype(F32) + t2_next[k, 0, at, :].astype(F32)
-            high = mid[k, 0, pl.ds(pl.multiple_of(rows + i * chunk, chunk), chunk), :].astype(F32) + t2_prev[k, 1, at, :].astype(F32) + t2_next[k, 1, at, :].astype(F32)
-            keep[k, at, :] = jnp.where(upper == 1, high, low)
-            z_send[k, at, :] = jnp.where(upper == 1, low, high).astype(BF16)
-            return carry
-
-        lax.fori_loop(0, rows // chunk, last_sum, 0)
+        add_up(rows, into_buf(z_send, k), lambda i, at: mid[k, 0, pl.ds(pl.multiple_of(rows + i * chunk, chunk), chunk), :].astype(F32), from_buf(t2_prev, k, 1), from_buf(t2_next, k, 1))
         one.zz.start()
+        add_up(rows, into_buf(keep, k), from_buf(mid, k, 0), from_buf(t2_prev, k, 0), from_buf(t2_next, k, 0))
     for one in sides:
         k = one.k
         one.zz.wait_recv()
@@ -452,33 +506,62 @@
             out_ref[at, k * half:(k + 1) * half] = total.astype(BF16)
 
         add_up(rows, store_out, from_buf(keep, k), from_buf(z_recv, k))
+
+    def last_tile(t):
+        core_msg(1, t).wait_recv()
+        far_msg(t).wait_recv()
+
+        def step(i, carry):
+            at = pl.ds(pl.multiple_of(t * tile + i * 32, 32), 32)
+            dx_ref[at, :] = (dx_part[0, at, :] + core_recv[1, at, :] + far_recv[at, :]).astype(BF16)
+            return carry
+
+        lax.fori_loop(0, tile // 32, step, 0)
+
+    tiles(last_tile)
+
+    def sent(t):
+        core_msg(0, t).wait_send()
+        core_msg(1, t).wait_send()
+        far_msg(t).wait_send()
+
+    tiles(sent)
     for one in sides:
         for msg in one.s1n + one.s1p + one.inn + one.inp + one.dpn + one.dpp + [one.t1n, one.t1p, one.tin, one.tip, one.tdn, one.tdp, one.zz]:
             msg.wait_send()
 
 
-def reduce_rows(part):
+def tail_pass(part, c_all, uc, y_own, y_core, y_far):
     width = part.shape[1]
     rows = part.shape[0] // N_OWN
+    n_tok = y_own.shape[0]
     half = width // 2
-    big, small = (2 * rows, half), (rows, half)
+    big, small, toks = (2 * rows, half), (rows, half), (n_tok, width)
     vmem = pl.BlockSpec(memory_space=pltpu.VMEM)
+    hbm = pl.BlockSpec(memory_space=pl.ANY)
+    dma = pltpu.SemaphoreType.DMA
     return pl.pallas_call(
-        reduce_kernel,
-        in_specs=[vmem],
-        out_specs=vmem,
-        out_shape=jax.ShapeDtypeStruct((rows, width), BF16),
-        scratch_shapes=[pltpu.VMEM(shape, BF16) for shape in ((2, 2, *big), (2, 2, *big), (2, 4, *big), (2, 4, *big), (2, 2, *big), (2, 2, *big), (2, 4, *big), (2, *small), (2, *small), (2, 2, *small), (2, 2, *small), (2, *small), (2, *small))]
-        + [pltpu.VMEM((2, *small), F32), pltpu.VMEM((2, *small), BF16), pltpu.VMEM((2, *small), BF16), pltpu.SemaphoreType.DMA((2, N_MSG)), pltpu.SemaphoreType.DMA((2, N_MSG))],
-        compiler_params=pltpu.CompilerParams(collective_id=0, has_side_effects=True, vmem_limit_bytes=48 * 2 ** 20),
-        cost_estimate=pl.CostEstimate(flops=10 ** 9, bytes_accessed=part.size * 4, transcendentals=0),
-        name="reduce_rows",
-    )(part)
-
-
-def hot_tables(req_sets, core, zgrp):
+        tail_kernel,
+        in_specs=[hbm] * 6,
+        out_specs=[vmem] * 3,
+        out_shape=[jax.ShapeDtypeStruct((rows, width), BF16), jax.ShapeDtypeStruct(toks, BF16), jax.ShapeDtypeStruct(toks, BF16)],
+        scratch_shapes=[pltpu.VMEM(shape, BF16) for shape in (
+            (2, 2, *big), (2, 2, *big), (2, 4, *big), (2, 2, *big), (2, 2, *big), (2, 4, *big), (2, 4, *big), (2, 2, *big), (2, 2, *big), (2, 4, *big),
+            (2, *small), (2, *small), (2, 2, *small), (2, 2, *small), (2, *small), (2, *small))]
+        + [pltpu.VMEM((2, *small), F32), pltpu.VMEM((2, *small), BF16), pltpu.VMEM((2, *small), BF16),
+           pltpu.VMEM((2, n_tok, N_GRP * 256), BF16), pltpu.VMEM((2, N_GRP, 256, width), BF16),
+           pltpu.VMEM((N_SET, *toks), F32), pltpu.VMEM((2, *toks), F32), pltpu.VMEM(toks, F32), pltpu.VMEM(toks, F32), pltpu.VMEM((3, *toks), F32),
+           dma((2, N_MSG)), dma((2, N_MSG)), dma((2, 8)), dma((N_SET, 2)), dma((3,)),
+           dma((2, N_TILE)), dma((2, N_TILE)), dma((N_TILE,)), dma((N_TILE,))],
+        compiler_params=pltpu.CompilerParams(collective_id=0, has_side_effects=True, vmem_limit_bytes=60 * 2 ** 20),
+        cost_estimate=pl.CostEstimate(flops=2 * N_SET * n_tok * N_GRP * 256 * width, bytes_accessed=40 * 2 ** 20, transcendentals=0),
+        name="tail_pass",
+    )(part, c_all, uc, y_own, y_core, y_far)
+
+
+def hot_tables(req_sets, core, z_me):
     yx = jnp.arange(16)[:, None]
-    z_of = jnp.where(zgrp == 0, jnp.array([0, 3]), jnp.array([1, 2]))[None, :]
+    z_of = jnp.stack([z_me, 3 - z_me])[None, :]
     owners = ((z_of * 16 + yx) * 2 + core).reshape(N_OWN)
     req = jnp.stack([one[owners] for one in req_sets], axis=1)
     req = req.reshape(N_GRP, 2, 2, N_SET, REQ).transpose(0, 3, 1, 2, 4)
@@ -502,25 +585,15 @@
         n_sel = slot_ids.shape[1] * slot_ids.shape[2]
         index = lax.axis_index('ep')
         core, z_me = index % 2, index // 32
-        zgrp = ((z_me + 1) // 2) % 2
 
         def table_rows(local):
-            other = swap(local, ZTAB)
-            both = jnp.where(z_me < 2, jnp.concatenate([local, other]), jnp.concatenate([other, local]))
+            both = jnp.concatenate([local, swap(local, ZTAB)])
             return lax.all_gather(both, 'ep', axis=0, tiled=True, axis_index_groups=plane)
 
-        def grad_rows(part):
+        def grad_rows(part, after):
             mine = lax.psum_scatter(part, 'ep', scatter_dimension=0, tiled=True, axis_index_groups=plane)
-            keep = lax.dynamic_slice_in_dim(mine, (z_me // 2) * ROWS, ROWS)
-            give = lax.dynamic_slice_in_dim(mine, (1 - z_me // 2) * ROWS, ROWS)
-            return (keep.astype(F32) + swap(give, ZTAB).astype(F32)).astype(BF16)
-
-        def for_other_chip(remote_part):
-            return remote_part[:n_tok] + swap(remote_part[n_tok:], CORE)
-
-        def collect(local_part, from_z):
-            from_core = swap(local_part[n_tok:], CORE)
-            return (local_part[:n_tok] + from_core + from_z).astype(BF16)
+            mine, _ = lax.optimization_barrier((mine, after))
+            return (mine[:ROWS].astype(F32) + swap(mine[ROWS:], ZTAB).astype(F32)).astype(BF16)
 
         n_req = request_rows.shape[1] * request_rows.shape[2] // n_sel
         meta0 = jnp.concatenate([slot_ids.reshape(n_tok, n_sel).astype(F32), gate_vals.reshape(n_tok, n_sel), request_rows.reshape(n_req, n_sel).astype(F32)])
@@ -534,23 +607,20 @@
         xs = (tokens, swap(tokens, CORE), x2, swap(x2, CORE))
         dys = (grad_out, swap(grad_out, CORE), dy2, swap(dy2, CORE))
         metas = (meta0, meta1, meta2, meta3)
-        p_hot, pt_hot = hot_tables([m[2 * n_tok:].reshape(N_EP, REQ).astype(jnp.int32) for m in metas], core, zgrp)
-
-        ctl = jnp.stack([core, zgrp]).astype(jnp.int32)
+        p_hot, pt_hot = hot_tables([m[2 * n_tok:].reshape(N_EP, REQ).astype(jnp.int32) for m in metas], core, z_me)
+
+        ctl = jnp.stack([core, z_me]).astype(jnp.int32)
         gates = []
         for meta in metas:
             gates.append(gate_matrix(ctl, meta, n_tok))
         uc, w_all, slopes, dv_part = first_pass(u_all, p_hot, pt_hot, gates, xs, dys)
-        vc, y_part = down_pass(v_all, p_hot, w_all)
-        y_for_z, vc = lax.optimization_barrier((for_other_chip(y_part[2 * n_tok:]), vc))
-        y_from_z = swap(y_for_z, ZTOK)
+        vc, *y_parts = down_pass(v_all, p_hot, w_all)
+        y_for_far, vc = lax.optimization_barrier((y_parts[2] + swap(y_parts[3], CORE), vc))
+        y_far = swap(y_for_far, ZTOK)
+        y_core = swap(y_parts[1], CORE)
         c_all, du_part = second_pass(vc, pt_hot, slopes, xs, dys)
-        dx_rem = token_grad(c_all, uc, 2)
-        dx_loc = token_grad(c_all, uc, 0)
-        y = collect(y_part[:2 * n_tok], y_from_z)
-        grad_down = grad_rows(dv_part)
-        grad_up = reduce_rows(du_part)
-        dx = collect(dx_loc, swap(for_other_chip(dx_rem), ZTOK))
+        grad_up, dx, y = tail_pass(du_part, c_all, uc, y_parts[0], y_core, y_far)
+        grad_down = grad_rows(dv_part, grad_up)
         return y, dx, grad_up, grad_down
 
     return jax.shard_map(device_part, mesh=mesh, in_specs=(tok_spec, tok_spec, tok_spec, tok_spec, tok_spec, table_spec, table_spec), out_specs=(tok_spec, tok_spec, tok_spec, tok_spec), check_vma=False)

time: 354 us -> 328 us (0.927)
  Pallas kernels: 221 us -> 208 us
  other arithmetic: 26.6 us -> 17.6 us
  local copies, waits for them, and re-layouts: 15.6 us -> 10.2 us
    pallas_call x3 -> x1, Pallas kernels: 75.4 us -> 62.6 us  [tail_pass(): pl.pallas_call(tail_kernel, in_specs=[hbm] * 6, out_specs=[vmem] * 3, out...]
    slice x3 -> x1, local copies, waits for them, and re-layouts: 10.8 us -> 1.01 us  [grad_rows(): mine[ROWS:]]
    convert_element_type x3 -> x1, other arithmetic: 9.54 us -> 1.72 us  [grad_rows(): (mine[:ROWS].astype(F32) + swap(mine[ROWS:], ZTAB).astype(F32)).astype(BF16)]
    unnamed x24 -> x20, local copies, waits for them, and re-layouts: 0.85 us -> 6.15 us
    select_n x2 -> x0, other arithmetic: 4 us -> none  [table_rows(): jnp.where(z_me < 2, jnp.concatenate([local, other]), jnp.concatenate([oth...]
    concatenate x0 -> x2, other arithmetic: none -> 3.56 us  [table_rows(): both = jnp.concatenate([local, swap(local, ZTAB)])]
    ppermute x18 -> x15, starting transfers between devices: 21.1 us -> 24 us  [swap(): return lax.ppermute(arr, 'ep', [(i, i ^ mask) for i in range(N_EP)])]
    ppermute x18 -> x15, waiting for transfers between devices: 46.9 us -> 45.9 us  [swap(): return lax.ppermute(arr, 'ep', [(i, i ^ mask) for i in range(N_EP)])]
  transfers between devices with their start and end apart: 21 -> 18, of which waited for: 6 -> 7; matrix products, arithmetic and copies ran while one was open for 11% -> 6% of each run, Pallas kernels for 63% -> 64%
where the time goes in v1:
time: 328 us; the launch traced here: 323 us
  Pallas kernels  208 us (63%)
  waiting for transfers between devices  49.4 us (15%)
  starting transfers between devices  24.1 us (7%)
  other arithmetic  17.6 us (5%)
  between operations  14 us (4%)
  local copies, waits for them, and re-layouts  10.2 us (3%)
    pallas_call x1, Pallas kernels, tail_pass(): pl.pallas_call(tail_kernel, in_specs=[hbm] * 6, out_specs=[vmem] * 3, out...  62.6 us
    pallas_call x1, Pallas kernels, first_pass(): pl.pallas_call(functools.partial(first_kernel, n_tok), grid=(N_GRP,), in_...  51.3 us
    ppermute x15, waiting for transfers between devices, swap(): return lax.ppermute(arr, 'ep', [(i, i ^ mask) for i in range(N_EP)])  45.9 us
    pallas_call x1, Pallas kernels, second_pass(): pl.pallas_call(functools.partial(second_kernel, n_tok), grid=(N_GRP,), in...  38.6 us
    pallas_call x4, Pallas kernels, gate_matrix(): pl.pallas_call(gate_kernel, grid=(n_blk,), in_specs=[pl.BlockSpec(memory_...  34.3 us
    ppermute x15, starting transfers between devices, swap(): return lax.ppermute(arr, 'ep', [(i, i ^ mask) for i in range(N_EP)])  24 us
    pallas_call x1, Pallas kernels, down_pass(): pl.pallas_call(functools.partial(down_kernel, n_tok), grid=(N_GRP,), in_s...  20.8 us
  transfers between devices with their start and end apart: 18, of which 7 were waited for; matrix products, arithmetic and copies ran while one was open for 6% of the time, Pallas kernels for 64%

profile of v1, /device:TPU:11, one launch (start us, length us, event | category | flops | bytes accessed | tf_op | source)
XLA Modules:
  0.0 323.0 jit_solution(15109098145686088435)
XLA Ops:
  7.2 0.0 all-gather.5.cloned.1.call-start
  7.2 3.8 %collective-permute-start.4 = (bf16[128,1024]{1,0:T(8,128)(2,1)}, bf16[128,1024]{1,0:T(8,128)(2,1)S(1)}, u32[]{:S(2)}, u32[]{:S(2)}) collective-permute-start(bf16[128,1024]{1,0:T(8,128)(2,1)} %param.12), channel_id=1, source_target_pairs={{0,96},{1,97},{2,98},{3,99},{4,100},{5,101},{6,102},{7,103},{8,104... | collective-permute-start | bytes 786440 | tf_op jit(solution)/shard_map/ppermute | solution.py:581
  11.1 6.2 %collective-permute-done.4 = bf16[128,1024]{1,0:T(8,128)(2,1)S(1)} collective-permute-done((bf16[128,1024]{1,0:T(8,128)(2,1)}, bf16[128,1024]{1,0:T(8,128)(2,1)S(1)}, u32[]{:S(2)}, u32[]{:S(2)}) %collective-permute-start.4) | collective-permute-done | bytes 262176 | tf_op jit(solution)/shard_map/ppermute | solution.py:581
  17.3 1.8 pad_maximum_fusion.2
  19.1 0.0 all-gather.5.cloned.1.call-update
  19.1 0.0 all-gather.3.cloned.1.call-start
  19.1 2.5 collective-permute-start
  21.6 5.6 %collective-permute-done = bf16[128,1024]{1,0:T(8,128)(2,1)S(1)} collective-permute-done((bf16[128,1024]{1,0:T(8,128)(2,1)}, bf16[128,1024]{1,0:T(8,128)(2,1)S(1)}, u32[]{:S(2)}, u32[]{:S(2)}) %collective-permute-start) | collective-permute-done | bytes 262176 | tf_op jit(solution)/shard_map/ppermute | solution.py:581
  27.3 1.8 pad_maximum_fusion.1
  29.1 0.0 reduce-scatter.2.cloned.1.call-start
  29.1 0.8 copy.15
  30.0 0.1 convert_element_type.58
  30.1 1.0 convert_element_type.56
  31.1 0.1 copy.16
  31.2 0.1 copy.17
  31.4 0.1 collective-permute-start.2
  31.5 2.2 collective-permute-start.1
  33.7 1.7 collective-permute-start.6
  35.3 0.3 collective-permute-start.5
  35.6 0.1 add_multiply_fusion
  35.7 0.7 pad_add_fusion.ctl_ref
  36.3 8.6 %gate_matrix.4.refs_0_ = f32[64,16,8,128]{3,2,1,0:T(8,128)} custom-call(s32[2]{0:T(128)} %pad_add_fusion.ctl_ref, f32[1088,128]{1,0:T(8,128)} %copy-done.1, f32[1088,128]{1,0:T(8,128)} %copy-done.1), custom_call_target="tpu_custom_call" | custom-call | flops 6442450944 | bytes 4718592 | tf_op jit(solution)/shard_map/gate_matrix/pallas_call | solution.py:84
  44.9 0.1 add.82
  45.0 0.6 gather_fusion
  45.6 3.4 %collective-permute-start.8 = (bf16[512,1024]{1,0:T(8,128)(2,1)}, bf16[512,1024]{1,0:T(8,128)(2,1)}, u32[]{:S(2)}, u32[]{:S(2)}) collective-permute-start(bf16[512,1024]{1,0:T(8,128)(2,1)} %refs_4_.3), channel_id=1, source_target_pairs={{0,1},{1,0},{2,3},{3,2},{4,5},{5,4},{6,7},{7,6},{8,9},{9,8},{10,11... | collective-permute-start | bytes 3145736 | tf_op jit(solution)/shard_map/ppermute | solution.py:581
  49.1 0.1 convert_element_type.62
  49.1 0.6 gather_fusion.2
  49.8 0.1 convert_element_type.60
  49.8 0.6 gather_fusion.1
  50.4 0.1 collective-permute-start.3
  50.5 0.0 copy-done.5
  50.5 8.6 %gate_matrix.5.refs_1_ = f32[64,16,8,128]{3,2,1,0:T(8,128)} custom-call(s32[2]{0:T(128)} %pad_add_fusion.ctl_ref, f32[1088,128]{1,0:T(8,128)} %copy-done.5, f32[1088,128]{1,0:T(8,128)} %copy-done.5), custom_call_target="tpu_custom_call" | custom-call | flops 6442450944 | bytes 4718592 | tf_op jit(solution)/shard_map/gate_matrix/pallas_call | solution.py:84
  59.1 8.6 %gate_matrix.6.refs_2_ = f32[64,16,8,128]{3,2,1,0:T(8,128)} custom-call(s32[2]{0:T(128)} %pad_add_fusion.ctl_ref, f32[1088,128]{1,0:T(8,128)} %copy-done.4, f32[1088,128]{1,0:T(8,128)} %copy-done.4), custom_call_target="tpu_custom_call" | custom-call | flops 6442450944 | bytes 4718592 | tf_op jit(solution)/shard_map/gate_matrix/pallas_call | solution.py:84
  67.7 3.9 %collective-permute-start.7 = (bf16[512,1024]{1,0:T(8,128)(2,1)}, bf16[512,1024]{1,0:T(8,128)(2,1)}, u32[]{:S(2)}, u32[]{:S(2)}) collective-permute-start(bf16[512,1024]{1,0:T(8,128)(2,1)} %collective-permute-done.6.refs_6_.refs_2_), channel_id=1, source_target_pairs={{0,1},{1,0},{2,3},{3,2},{4,5},{5,4},{6,7},{7,6},{8,9},{9,8},{10,11... | collective-permute-start | bytes 3145736 | tf_op jit(solution)/shard_map/ppermute | solution.py:581
  71.6 17.0 %collective-permute-done.9.refs_10_.refs_6_ = bf16[512,1024]{1,0:T(8,128)(2,1)} collective-permute-done((bf16[512,1024]{1,0:T(8,128)(2,1)}, bf16[512,1024]{1,0:T(8,128)(2,1)}, u32[]{:S(2)}, u32[]{:S(2)}) %collective-permute-start.9) | collective-permute-done | bytes 1048608 | tf_op jit(solution)/shard_map/ppermute | solution.py:581
  88.6 3.0 collective-permute-start.10
  91.6 0.1 convert_element_type.64
  91.6 0.6 gather_fusion.3
  92.2 0.1 fusion.2
  92.3 0.1 reshape.137
  92.4 3.4 %fusion.1.pt_ref = bf16[8,4,2,256,128]{4,3,2,1,0:T(8,128)(2,1)} fusion(s32[8,4,2,128]{3,2,1,0:T(2,128)S(1)} %copy.22), kind=kLoop, calls=%fused_computation.7 | loop fusion | flops 4194304 | bytes 4227072 | tf_op jit(solution)/shard_map/convert_element_type | solution.py:570
  95.8 3.7 %fusion.p_ref = bf16[8,2,512,256]{3,2,1,0:T(8,128)(2,1)} fusion(s32[8,2,512]{2,1,0:T(2,128)S(1)} %bitcast.22), kind=kLoop, calls=%fused_computation.6 | loop fusion | flops 4194304 | bytes 4227072 | tf_op jit(solution)/shard_map/convert_element_type | solution.py:571
  99.5 8.6 %gate_matrix.7.refs_3_ = f32[64,16,8,128]{3,2,1,0:T(8,128)} custom-call(s32[2]{0:T(128)} %pad_add_fusion.ctl_ref, f32[1088,128]{1,0:T(8,128)} %copy-done.6, f32[1088,128]{1,0:T(8,128)} %copy-done.6), custom_call_target="tpu_custom_call" | custom-call | flops 6442450944 | bytes 4718592 | tf_op jit(solution)/shard_map/gate_matrix/pallas_call | solution.py:84
  108.2 0.0 all-gather.5.cloned.1.call-done.u_ref
  108.2 51.3 %first_pass.1 = (bf16[8,4,256,1024]{3,2,1,0:T(8,128)(2,1)}, bf16[2048,2048]{1,0:T(8,128)(2,1)}, f32[2048,2048]{1,0:T(8,128)}, bf16[4096,1024]{1,0:T(8,128)(2,1)}) custom-call(bf16[4096,1024]{1,0:T(8,128)(2,1)} %all-gather.5.cloned.1.call-done.u_ref, bf16[8,2,512,256]{3,2,1,0:T(8,128)(2,1)} %fusion.p_ref, bf16[8,4,2,256,128]{4,3,2,1,0:T(8,128)(2,1)} %fusion.1.pt_ref, ...), custom_call_target="tpu_custom_call" | custom-call | flops 32212254720 | bytes 79691776 | tf_op jit(solution)/shard_map/first_pass/pallas_call | solution.py:152
  159.5 0.0 reduce-scatter.2.cloned.1.call-update
  159.5 3.3 %all-gather.3.cloned.1.call-done.v_ref = bf16[4096,1024]{1,0:T(8,128)(2,1)} async-done(((bf16[256,1024]{1,0:T(8,128)(2,1)}), bf16[4096,1024]{1,0:T(8,128)(2,1)}) %all-gather.3.cloned.1.call-update) | async-done | bytes 8388624 | tf_op jit(solution)/shard_map/all_gather | solution.py:591
  162.8 20.8 %down_pass.1 = (bf16[8,4,256,1024]{3,2,1,0:T(8,128)(2,1)}, f32[512,1024]{1,0:T(8,128)}, f32[512,1024]{1,0:T(8,128)}, f32[512,1024]{1,0:T(8,128)}, f32[512,1024]{1,0:T(8,128)}) custom-call(bf16[4096,1024]{1,0:T(8,128)(2,1)} %all-gather.3.cloned.1.call-done.v_ref, bf16[8,2,512,256]{3,2,1,0:T(8,128)(2,1)} %fusion.p_ref, bf16[2048,2048]{1,0:T(8,128)(2,1)} %get-tuple-element.21.w_ref), custom_call_target="tpu_custom_call" | custom-call | flops 12884901888 | bytes 46137344 | tf_op jit(solution)/shard_map/down_pass/pallas_call | solution.py:195
  183.7 0.4 collective-permute-start.11
  184.1 0.1 collective-permute-start.12
  184.2 3.9 %collective-permute-done.11 = f32[512,1024]{1,0:T(8,128)S(1)} collective-permute-done((f32[512,1024]{1,0:T(8,128)}, f32[512,1024]{1,0:T(8,128)S(1)}, u32[]{:S(2)}, u32[]{:S(2)}) %collective-permute-start.11) | collective-permute-done | bytes 2097184 | tf_op jit(solution)/shard_map/ppermute | solution.py:581
  188.0 3.3 %add.87 = f32[512,1024]{1,0:T(8,128)} add(f32[512,1024]{1,0:T(8,128)} %get-tuple-element.22, f32[512,1024]{1,0:T(8,128)S(1)} %collective-permute-done.11) | non-fusion elementwise | flops 524288 | bytes 6291456 | tf_op jit(solution)/shard_map/add | solution.py:618
  191.4 1.3 collective-permute-start.13
  192.7 38.6 %second_pass.1 = (bf16[2048,2048]{1,0:T(8,128)(2,1)}, bf16[4096,1024]{1,0:T(8,128)(2,1)}) custom-call(bf16[8,4,256,1024]{3,2,1,0:T(8,128)(2,1)} %get-tuple-element.25.vc_ref, bf16[8,4,2,256,128]{4,3,2,1,0:T(8,128)(2,1)} %fusion.1.pt_ref, f32[2048,2048]{1,0:T(8,128)} %get-tuple-element.26.s_ref, bf16[512,1024]{1,0:T(8,128)(2,1)} %refs_0_.1, ...), custom_call_target="tpu_custom_call" | custom-call | flops 27917287424 | bytes 60817408 | tf_op jit(solution)/shard_map/second_pass/pallas_call | solution.py:244
  231.3 7.2 %collective-permute-done.13.yz_ref = f32[512,1024]{1,0:T(8,128)} collective-permute-done((f32[512,1024]{1,0:T(8,128)}, f32[512,1024]{1,0:T(8,128)}, u32[]{:S(2)}, u32[]{:S(2)}) %collective-permute-start.13) | collective-permute-done | bytes 2097184 | tf_op jit(solution)/shard_map/ppermute | solution.py:581
  238.5 62.6 %tail_pass.1 = (bf16[128,1024]{1,0:T(8,128)(2,1)}, bf16[512,1024]{1,0:T(8,128)(2,1)}, bf16[512,1024]{1,0:T(8,128)(2,1)}) custom-call(bf16[4096,1024]{1,0:T(8,128)(2,1)} %get-tuple-element.27.part_ref, bf16[2048,2048]{1,0:T(8,128)(2,1)} %get-tuple-element.28.c_ref, bf16[8,4,256,1024]{3,2,1,0:T(8,128)(2,1)} %get-tuple-element.29.uc_ref, ...), custom_call_target="tpu_custom_call" | custom-call | flops 8589934592 | bytes 41943040 | tf_op jit(solution)/shard_map/tail_pass/pallas_call | solution.py:543
  301.2 0.0 reduce-scatter.2.cloned.1.call-done
  301.2 1.0 slice.19
  302.2 1.3 collective-permute-start.14
  303.5 6.0 %collective-permute-done.14 = bf16[128,1024]{1,0:T(8,128)(2,1)S(1)} collective-permute-done((bf16[128,1024]{1,0:T(8,128)(2,1)S(1)}, bf16[128,1024]{1,0:T(8,128)(2,1)S(1)}, u32[]{:S(2)}, u32[]{:S(2)}) %collective-permute-start.14) | collective-permute-done | bytes 262176 | tf_op jit(solution)/shard_map/ppermute | solution.py:581
  309.5 1.7 add_convert_fusion
  311.2 2.3 copy.26
  313.5 2.3 copy.27
  315.7 0.7 copy.28
  (36 shorter events, 0.2 us)
Async XLA Ops:
  7.2 24.0 %copy-start.2 = (f32[512,4,32]{0,2,1:T(8,128)S(1)}, f32[512,4,32]{0,2,1:T(8,128)}, u32[]{:S(2)}) copy-start(f32[512,4,32]{0,2,1:T(8,128)} %param.10) | copy-start | bytes 786436
  7.2 26.5 %copy-start.7 = (bf16[512,1024]{1,0:T(8,128)(2,1)S(1)}, bf16[512,1024]{1,0:T(8,128)(2,1)}, u32[]{:S(2)}) copy-start(bf16[512,1024]{1,0:T(8,128)(2,1)} %refs_0_.1) | copy-start | bytes 3145732
  7.2 101.0 %all-gather.5.cloned.1.call-start = ((), (), s32[]{:S(2)}) async-start(), calls=%async_computation.2 | async-start | bytes 8912896 | tf_op jit(solution)/shard_map/all_gather | solution.py:591
  7.2 10.1 %collective-permute-start.4 = (bf16[128,1024]{1,0:T(8,128)(2,1)}, bf16[128,1024]{1,0:T(8,128)(2,1)S(1)}, u32[]{:S(2)}, u32[]{:S(2)}) collective-permute-start(bf16[128,1024]{1,0:T(8,128)(2,1)} %param.12), channel_id=1, source_target_pairs={{0,96},{1,97},{2,98},{3,99},{4,100},{5,101},{6,102},{7,103},{8,104... | collective-permute-start | bytes 786440 | tf_op jit(solution)/shard_map/ppermute | solution.py:581
  19.1 143.7 %all-gather.3.cloned.1.call-start = ((), (), s32[]{:S(2)}) async-start(), calls=%async_computation.1 | async-start | bytes 8912896 | tf_op jit(solution)/shard_map/all_gather | solution.py:591
  19.1 8.1 %collective-permute-start = (bf16[128,1024]{1,0:T(8,128)(2,1)}, bf16[128,1024]{1,0:T(8,128)(2,1)S(1)}, u32[]{:S(2)}, u32[]{:S(2)}) collective-permute-start(bf16[128,1024]{1,0:T(8,128)(2,1)} %param.13), channel_id=1, source_target_pairs={{0,96},{1,97},{2,98},{3,99},{4,100},{5,101},{6,102},{7,103},{8,104... | collective-permute-start | bytes 786440 | tf_op jit(solution)/shard_map/ppermute | solution.py:581
  29.1 272.1 %reduce-scatter.2.cloned.1.call-start = ((), (), s32[]{:S(2)}) async-start(), calls=%async_computation.3 | async-start | bytes 8912896 | tf_op jit(solution)/shard_map/reduce_scatter | solution.py:594
  31.4 5.0 %copy-start.1 = (f32[1088,128]{1,0:T(8,128)}, f32[1088,128]{1,0:T(8,128)S(1)}, u32[]{:S(2)}) copy-start(f32[1088,128]{1,0:T(8,128)S(1)} %pad_maximum_fusion.slot_ref.gate_ref) | copy-start | bytes 1671172
  31.4 14.2 %collective-permute-start.2 = (f32[1088,128]{1,0:T(8,128)S(1)}, f32[1088,128]{1,0:T(8,128)S(1)}, u32[]{:S(2)}, u32[]{:S(2)}) collective-permute-start(f32[1088,128]{1,0:T(8,128)S(1)} %pad_maximum_fusion.slot_ref.gate_ref), channel_id=1, source_target_pairs={{0,32},{1,33},{2,34},{3,35},{4,36},{5,37},{6,38},{7,39},{8,40},{9,... | collective-permute-start | bytes 1671176 | tf_op jit(solution)/shard_map/ppermute | solution.py:581
  31.5 18.2 %collective-permute-start.1 = (f32[1088,128]{1,0:T(8,128)S(1)}, f32[1088,128]{1,0:T(8,128)S(1)}, u32[]{:S(2)}, u32[]{:S(2)}) collective-permute-start(f32[1088,128]{1,0:T(8,128)S(1)} %pad_maximum_fusion.slot_ref.gate_ref), channel_id=1, source_target_pairs={{0,1},{1,0},{2,3},{3,2},{4,5},{5,4},{6,7},{7,6},{8,9},{9,8},{10,11... | collective-permute-start | bytes 1671176 | tf_op jit(solution)/shard_map/ppermute | solution.py:581
  33.7 34.1 %collective-permute-start.6 = (bf16[512,1024]{1,0:T(8,128)(2,1)S(1)}, bf16[512,1024]{1,0:T(8,128)(2,1)}, u32[]{:S(2)}, u32[]{:S(2)}) collective-permute-start(bf16[512,1024]{1,0:T(8,128)(2,1)S(1)} %copy-done.7), channel_id=1, source_target_pairs={{0,32},{1,33},{2,34},{3,35},{4,36},{5,37},{6,38},{7,39},{8,40},{9,... | collective-permute-start | bytes 3145736 | tf_op jit(solution)/shard_map/ppermute | solution.py:581
  35.3 72.8 %collective-permute-start.5 = (bf16[512,1024]{1,0:T(8,128)(2,1)S(1)}, bf16[512,1024]{1,0:T(8,128)(2,1)}, u32[]{:S(2)}, u32[]{:S(2)}) collective-permute-start(bf16[512,1024]{1,0:T(8,128)(2,1)S(1)} %copy-done.7), channel_id=1, source_target_pairs={{0,1},{1,0},{2,3},{3,2},{4,5},{5,4},{6,7},{7,6},{8,9},{9,8},{10,11... | collective-permute-start | bytes 3145736 | tf_op jit(solution)/shard_map/ppermute | solution.py:581
  35.6 53.0 %collective-permute-start.9 = (bf16[512,1024]{1,0:T(8,128)(2,1)}, bf16[512,1024]{1,0:T(8,128)(2,1)}, u32[]{:S(2)}, u32[]{:S(2)}) collective-permute-start(bf16[512,1024]{1,0:T(8,128)(2,1)} %refs_4_.3), channel_id=1, source_target_pairs={{0,32},{1,33},{2,34},{3,35},{4,36},{5,37},{6,38},{7,39},{8,40},{9,... | collective-permute-start | bytes 3145736 | tf_op jit(solution)/shard_map/ppermute | solution.py:581
  45.6 13.5 %copy-start.4 = (f32[1088,128]{1,0:T(8,128)}, f32[1088,128]{1,0:T(8,128)S(1)}, u32[]{:S(2)}) copy-start(f32[1088,128]{1,0:T(8,128)S(1)} %collective-permute-done.2.slot_ref.gate_ref) | copy-start | bytes 1671172
  45.6 62.5 %collective-permute-start.8 = (bf16[512,1024]{1,0:T(8,128)(2,1)}, bf16[512,1024]{1,0:T(8,128)(2,1)}, u32[]{:S(2)}, u32[]{:S(2)}) collective-permute-start(bf16[512,1024]{1,0:T(8,128)(2,1)} %refs_4_.3), channel_id=1, source_target_pairs={{0,1},{1,0},{2,3},{3,2},{4,5},{5,4},{6,7},{7,6},{8,9},{9,8},{10,11... | collective-permute-start | bytes 3145736 | tf_op jit(solution)/shard_map/ppermute | solution.py:581
  49.7 0.8 copy-start.5
  50.4 41.1 %collective-permute-start.3 = (f32[1088,128]{1,0:T(8,128)S(1)}, f32[1088,128]{1,0:T(8,128)S(1)}, u32[]{:S(2)}, u32[]{:S(2)}) collective-permute-start(f32[1088,128]{1,0:T(8,128)S(1)} %collective-permute-done.2.slot_ref.gate_ref), channel_id=1, source_target_pairs={{0,1},{1,0},{2,3},{3,2},{4,5},{5,4},{6,7},{7,6},{8,9},{9,8},{10,11... | collective-permute-start | bytes 1671176 | tf_op jit(solution)/shard_map/ppermute | solution.py:581
  67.7 40.4 %collective-permute-start.7 = (bf16[512,1024]{1,0:T(8,128)(2,1)}, bf16[512,1024]{1,0:T(8,128)(2,1)}, u32[]{:S(2)}, u32[]{:S(2)}) collective-permute-start(bf16[512,1024]{1,0:T(8,128)(2,1)} %collective-permute-done.6.refs_6_.refs_2_), channel_id=1, source_target_pairs={{0,1},{1,0},{2,3},{3,2},{4,5},{5,4},{6,7},{7,6},{8,9},{9,8},{10,11... | collective-permute-start | bytes 3145736 | tf_op jit(solution)/shard_map/ppermute | solution.py:581
  88.6 19.6 %collective-permute-start.10 = (bf16[512,1024]{1,0:T(8,128)(2,1)}, bf16[512,1024]{1,0:T(8,128)(2,1)}, u32[]{:S(2)}, u32[]{:S(2)}) collective-permute-start(bf16[512,1024]{1,0:T(8,128)(2,1)} %collective-permute-done.9.refs_10_.refs_6_), channel_id=1, source_target_pairs={{0,1},{1,0},{2,3},{3,2},{4,5},{5,4},{6,7},{7,6},{8,9},{9,8},{10,11... | collective-permute-start | bytes 3145736 | tf_op jit(solution)/shard_map/ppermute | solution.py:581
  91.6 8.0 %copy-start.6 = (f32[1088,128]{1,0:T(8,128)}, f32[1088,128]{1,0:T(8,128)S(1)}, u32[]{:S(2)}) copy-start(f32[1088,128]{1,0:T(8,128)S(1)} %collective-permute-done.3.slot_ref.gate_ref) | copy-start | bytes 1671172
  183.7 4.4 %collective-permute-start.11 = (f32[512,1024]{1,0:T(8,128)}, f32[512,1024]{1,0:T(8,128)S(1)}, u32[]{:S(2)}, u32[]{:S(2)}) collective-permute-start(f32[512,1024]{1,0:T(8,128)} %get-tuple-element.23), channel_id=1, source_target_pairs={{0,1},{1,0},{2,3},{3,2},{4,5},{5,4},{6,7},{7,6},{8,9},{9,8},{10,11... | collective-permute-start | bytes 6291464 | tf_op jit(solution)/shard_map/ppermute | solution.py:581
  184.1 47.2 %collective-permute-start.12 = (f32[512,1024]{1,0:T(8,128)}, f32[512,1024]{1,0:T(8,128)S(1)}, u32[]{:S(2)}, u32[]{:S(2)}) collective-permute-start(f32[512,1024]{1,0:T(8,128)} %get-tuple-element.31), channel_id=1, source_target_pairs={{0,1},{1,0},{2,3},{3,2},{4,5},{5,4},{6,7},{7,6},{8,9},{9,8},{10,11... | collective-permute-start | bytes 6291464 | tf_op jit(solution)/shard_map/ppermute | solution.py:581
  191.4 47.1 %collective-permute-start.13 = (f32[512,1024]{1,0:T(8,128)}, f32[512,1024]{1,0:T(8,128)}, u32[]{:S(2)}, u32[]{:S(2)}) collective-permute-start(f32[512,1024]{1,0:T(8,128)} %add.87), channel_id=1, source_target_pairs={{0,32},{1,33},{2,34},{3,35},{4,36},{5,37},{6,38},{7,39},{8,40},{9,... | collective-permute-start | bytes 6291464 | tf_op jit(solution)/shard_map/ppermute | solution.py:581
  231.3 7.2 %copy-start = (f32[512,1024]{1,0:T(8,128)}, f32[512,1024]{1,0:T(8,128)S(1)}, u32[]{:S(2)}) copy-start(f32[512,1024]{1,0:T(8,128)S(1)} %collective-permute-done.12.yc_ref) | copy-start | bytes 6291460
  301.1 14.6 %copy-start.3 = (bf16[128,1024]{1,0:T(8,128)(2,1)S(1)}, bf16[128,1024]{1,0:T(8,128)(2,1)}, u32[]{:S(2)}) copy-start(bf16[128,1024]{1,0:T(8,128)(2,1)} %get-tuple-element.48) | copy-start | bytes 786436
  302.2 7.3 %collective-permute-start.14 = (bf16[128,1024]{1,0:T(8,128)(2,1)S(1)}, bf16[128,1024]{1,0:T(8,128)(2,1)S(1)}, u32[]{:S(2)}, u32[]{:S(2)}) collective-permute-start(bf16[128,1024]{1,0:T(8,128)(2,1)S(1)} %slice.19), channel_id=1, source_target_pairs={{0,96},{1,97},{2,98},{3,99},{4,100},{5,101},{6,102},{7,103},{8,104... | collective-permute-start | bytes 786440 | tf_op jit(solution)/shard_map/ppermute | solution.py:581
Sparse Core Ops, SparseCore 0:
  19.2 70.9 all-gather.4
  92.4 70.3 all-gather.2
  166.2 87.0 reduce-scatter.1
